TPU v7x, 256 devices: a whole 4x4x8 slice. The times are simulated.
256 devices in a mesh: prow: 8 (over x_lo, y), pcol: 32 (over z, x_hi, core).
Axes of the slice: x: 4 (x_hi: 2, x_lo: 2; x = x_hi * 2 + x_lo), y: 4, z: 8, core: 2. Of those that a mesh axis runs over, the one named last changes fastest.
Arguments:
- inverse_factor: float32 [1024, 1024], P('pcol'), as said below
- diag_block: float32 [1024, 1024], P('pcol'), as said below
- panel_matrix: float32 [16, 8, 128, 1024], P(None, 'prow', 'pcol'), may hold values from -6 to 6
- panel_factor: float32 [16, 8, 128, 1024], P(None, 'prow', 'pcol'), may hold values from -0.1875 to 0.1875
- trailing: float32 [16, 8, 128, 4, 32, 128], P(None, 'prow', None, None, 'pcol'), may hold values from -6 to 6
Outputs:
- reduced_diag: float32 [1024, 1024], P('pcol')
- panel_result: float32 [16, 8, 128, 1024], P(None, 'prow', 'pcol')
- trailing_out: float32 [16, 8, 128, 4, 32, 128], P(None, 'prow', None, None, 'pcol')
Inputs may be any that keep to these rules, and one draw needn't show every extreme that they name: `inverse_factor`: lower triangular, diagonal entries between 0.5 and 2. `diag_block`: symmetric.
All inputs are finite; a program needn't handle non-finite values.
Results may differ from a plain program's by a relative error of at most 0.0003.
Values sent between devices are 32-bit elements; how exact they have to be, the bound alone decides.
A program may use at most 128 MiB of HBM per device.

v0:
```python
import jax
import jax.numpy as jnp
from jax import lax
from jax.sharding import Mesh
from jax.sharding import PartitionSpec as P

PCOL = ("pcol_0", "pcol_1", "pcol_2")


def joined_along(parts, dim):
    lengths = list(parts.shape[1:])
    lengths[dim] *= parts.shape[0]
    return jnp.moveaxis(parts, 0, dim).reshape(lengths)


def gather_in_order(array, axes, order):
    parts = array[None]
    for k in order:
        parts = lax.all_gather(parts, axes[k], axis=0, tiled=True)
    current = [lax.axis_size(axes[k]) for k in reversed(order)]
    parts = parts.reshape(*current, *array.shape)
    turned = sorted(range(len(order)), key=lambda place: order[len(order) - 1 - place])
    return parts.transpose(*turned, *range(len(order), parts.ndim)).reshape(-1, *array.shape)


def gather_axes(array, axes, order, dim):
    return joined_along(gather_in_order(array, axes, order), dim)


def in_one_piece(arrays, axis, dim, along):
    ends, at = ([], 0)
    for a in arrays[:-1]:
        at += a.shape[along]
        ends.append(at)
    both = jnp.concatenate(arrays, axis=along)
    return tuple(jnp.split(lax.all_gather(both, axis, axis=dim, tiled=True), ends, axis=along))


def broadcast(array, axis, root):
    mine = lax.axis_index(axis) == root
    return lax.psum(jnp.where(mine, array, jnp.zeros_like(array)), axis)


def body(inverse_factor, diag_block, panel_matrix, panel_factor, trailing):
    exact = lax.Precision.HIGHEST
    grid_rows = lax.axis_size("prow")
    grid_cols = lax.axis_size(PCOL)
    column = lax.axis_index(PCOL)
    grid_row = lax.axis_index("prow")
    local_rows = inverse_factor.shape[0]
    width = inverse_factor.shape[1]
    inverse_full = gather_axes(inverse_factor, PCOL, (1, 0, 2), 0)
    diag_terms = jnp.dot(
        diag_block, inverse_full.T, precision=exact, preferred_element_type=jnp.float32
    )
    terms_full = gather_axes(diag_terms, PCOL, (1, 0, 2), 0)
    reduced = jnp.dot(inverse_full, terms_full, precision=exact, preferred_element_type=jnp.float32)
    reduced_rows = lax.dynamic_slice_in_dim(reduced, column * local_rows, local_rows, 0)
    shape = panel_matrix.shape
    solved = jnp.dot(
        panel_matrix.reshape(-1, width),
        inverse_full.T,
        precision=exact,
        preferred_element_type=jnp.float32,
    )
    coupled = jnp.dot(
        panel_factor.reshape(-1, width),
        reduced,
        precision=exact,
        preferred_element_type=jnp.float32,
    )
    shifted = solved - 0.5 * coupled
    panel_result = (shifted - 0.5 * coupled).reshape(shape)
    rows_w, rows_l = in_one_piece((solved.reshape(shape), panel_factor), PCOL, 2, 0)
    again = jnp.dot(
        rows_l.reshape(-1, width), reduced, precision=exact, preferred_element_type=jnp.float32
    )
    rows_y = rows_w - 0.5 * again.reshape(rows_w.shape)
    tile_rows = rows_y.shape[0]
    tile = rows_y.shape[2]
    col_tiles = trailing.shape[3]
    stride = grid_cols // grid_rows
    picked = column // grid_rows

    def select(rows):
        grouped = rows.reshape(col_tiles, stride, tile, width)
        return lax.dynamic_index_in_dim(grouped, picked, 1, keepdims=False)

    col_y, col_l = (
        broadcast(select(rows_y), "prow", column % grid_rows),
        broadcast(select(rows_l), "prow", column % grid_rows),
    )
    rows_y = rows_y.reshape(tile_rows, tile, width)
    rows_l = rows_l.reshape(tile_rows, tile, width)
    block = trailing.reshape(tile_rows, tile, col_tiles, tile)
    row_ids = jnp.arange(tile_rows, dtype=jnp.int32) * grid_rows + grid_row
    col_ids = jnp.arange(col_tiles, dtype=jnp.int32) * grid_cols + column
    lower = (row_ids[:, None] >= col_ids[None, :])[:, None, :, None]
    update = jnp.einsum(
        "isk,jtk->isjt", rows_y, col_l, precision=exact, preferred_element_type=jnp.float32
    )
    update = update + jnp.einsum(
        "isk,jtk->isjt", rows_l, col_y, precision=exact, preferred_element_type=jnp.float32
    )
    result = jnp.where(lower, block - update, block)
    return (reduced_rows, panel_result, result.reshape(trailing.shape))


def solution(mesh):
    split = Mesh(
        mesh.devices.reshape(mesh.shape["prow"], 8, 2, 2), ("prow", "pcol_0", "pcol_1", "pcol_2")
    )
    return jax.shard_map(
        body,
        mesh=split,
        in_specs=(
            P(PCOL, None),
            P(PCOL, None),
            P(None, "prow", PCOL, None),
            P(None, "prow", PCOL, None),
            P(None, "prow", None, None, PCOL, None),
        ),
        out_specs=(
            P(PCOL, None),
            P(None, "prow", PCOL, None),
            P(None, "prow", None, None, PCOL, None),
        ),
        check_vma=False,
    )
```

profile of v0, /device:TPU:15, one launch (start us, length us, event | category | flops | bytes accessed | tf_op | source)
XLA Modules:
  0.0 510.8 jit_solution(1423629621830769323)
XLA Ops:
  7.2 0.0 copy-start
  7.2 0.0 all-gather.8.cloned.1.call-start
  7.2 6.9 %all-gather = f32[64,1024]{1,0:T(8,128)} all-gather(f32[32,1024]{1,0:T(8,128)} %param.5), channel_id=2, replica_groups=mesh['prow'=8,'pcol_0'=8,'pcol_1'=2,'pcol_2'=2] {'pcol_1'}, dimensions={0}, use_global_device_ids=true | all-gather | bytes 393216 | tf_op jit(solution)/shard_map/all_gather | solution.py:19
  14.1 0.0 all-gather.8.cloned.1.call-update
  14.1 0.0 all-gather.10.cloned.1.call-start
  14.2 40.4 %all-gather.8.cloned.1.call-done = f32[16,32,1024]{2,1,0:T(8,128)} async-done(((f32[2,32,1024]{2,1,0:T(8,128)}), f32[16,32,1024]{2,1,0:T(8,128)}) %all-gather.8.cloned.1.call-update) | async-done | bytes 2097168 | tf_op jit(solution)/shard_map/all_gather | solution.py:19
  54.6 0.0 all-gather.10.cloned.1.call-update
  54.6 0.0 all-gather.12.cloned.1.call-start
  54.7 24.0 %all-gather.10.cloned.1.call-done = f32[32,32,1024]{2,1,0:T(8,128)} async-done(((f32[16,32,1024]{2,1,0:T(8,128)}), f32[32,32,1024]{2,1,0:T(8,128)}) %all-gather.10.cloned.1.call-update) | async-done | bytes 4194320 | tf_op jit(solution)/shard_map/all_gather | solution.py:19
  78.6 2.5 copy.31
  81.1 0.0 copy-start.3
  81.2 2.0 copy-done.3
  83.2 3.9 fusion.24
  87.1 7.1 %all-gather.1 = f32[64,1024]{1,0:T(8,128)} all-gather(f32[32,1024]{1,0:T(8,128)S(1)} %fusion.24), channel_id=3, replica_groups=mesh['prow'=8,'pcol_0'=8,'pcol_1'=2,'pcol_2'=2] {'pcol_1'}, dimensions={0}, use_global_device_ids=true | all-gather | bytes 393216 | tf_op jit(solution)/shard_map/all_gather | solution.py:19
  94.2 0.0 all-gather.12.cloned.1.call-update
  94.2 0.0 all-gather.14.cloned.1.call-start
  94.2 38.5 %all-gather.12.cloned.1.call-done = f32[16,32,1024]{2,1,0:T(8,128)} async-done(((f32[2,32,1024]{2,1,0:T(8,128)}), f32[16,32,1024]{2,1,0:T(8,128)}) %all-gather.12.cloned.1.call-update) | async-done | bytes 2097168 | tf_op jit(solution)/shard_map/all_gather | solution.py:19
  132.7 0.0 all-gather.14.cloned.1.call-update
  132.7 0.0 all-gather.16.cloned.1.call-start
  132.8 0.1 reshape.90
  132.9 0.2 copy.35
  133.1 6.3 %fusion.26 = f32[64,1024]{1,0:T(8,128)S(1)} fusion(f32[64,1024]{1,0:T(8,128)S(1)} %reshape.90, f32[1024,1024]{1,0:T(8,128)} %bitcast.77), kind=kOutput, calls=%fused_computation.29 | convolution fusion | flops 805306368 | bytes 4718592 | tf_op jit(solution)/shard_map/dot_general | solution.py:60
  139.3 0.1 reshape.94
  139.4 0.2 copy.34
  139.6 0.9 pad_maximum_fusion
  140.4 0.0 all-gather.16.cloned.1.call-update
  140.4 0.0 all-reduce.3.cloned.1.call-start
  140.5 16.1 %all-gather.14.cloned.1.call-done = f32[32,32,1024]{2,1,0:T(8,128)} async-done(((f32[16,32,1024]{2,1,0:T(8,128)}), f32[32,32,1024]{2,1,0:T(8,128)}) %all-gather.14.cloned.1.call-update) | async-done | bytes 4194320 | tf_op jit(solution)/shard_map/all_gather | solution.py:19
  156.6 2.9 copy.32
  159.5 0.5 copy-done.4
  160.0 15.1 %fusion.25 = f32[1024,1024]{0,1:T(8,128)} fusion(f32[1024,1024]{1,0:T(8,128)S(1)} %bitcast.83, f32[1024,1024]{1,0:T(8,128)S(1)} %bitcast.78), kind=kOutput, calls=%fused_computation.28 | convolution fusion | flops 12884901888 | bytes 12582912 | tf_op jit(solution)/shard_map/dot_general | solution.py:57
  175.1 121.0 %all-gather.16.cloned.1.call-done = f32[32,1,128,1024]{3,0,1,2:T(8,128)} async-done(((f32[32,1,4,1024]{3,0,1,2:T(8,128)}), f32[32,1,128,1024]{3,0,1,2:T(8,128)}) %all-gather.16.cloned.1.call-update) | async-done | bytes 16777232 | tf_op jit(solution)/shard_map/all_gather | solution.py:36
  296.2 9.4 %fusion.23 = (f32[16,1,128,1024]{3,0,1,2:T(8,128)S(1)}, f32[16,1,128,1024]{3,0,1,2:T(8,128)}) fusion(f32[32,1,128,1024]{3,0,1,2:T(8,128)} %all-gather.16.cloned.1.call-done), kind=kLoop, calls=%fused_computation.26 | loop fusion | bytes 33554432 | tf_op jit(solution)/shard_map/split | solution.py:36
  305.6 4.9 copy.48
  310.4 0.3 copy-done.7
  310.8 37.9 %copy_subtract_fusion = f32[16,1,128,1024]{3,2,0,1:T(8,128)S(1)} fusion(f32[16,1,128,1024]{3,0,1,2:T(8,128)} %get-tuple-element.18, f32[1024,1024]{0,1:T(8,128)S(1)} %copy-done.7, f32[16,1,128,1024]{3,0,1,2:T(8,128)S(1)} %get-tuple-element.17), kind=kOutput, calls=%fused_computation | convolution fusion | flops 25773998080 | bytes 29360128 | tf_op jit(solution)/shard_map/dot_general | solution.py:75
  348.7 2.7 fusion.12
  351.4 1.8 copy-done.5
  353.2 0.0 all-reduce.3.cloned.1.call-update
  353.3 0.1 reshape.91
  353.4 0.1 broadcast_compare_fusion
  353.5 4.9 subtract_subtract_fusion
  358.4 0.8 reshape.92
  359.2 1.6 dynamic-slice_bitcast_fusion
  360.8 98.7 %all-reduce.3.cloned.1.call-done = (f32[4,128,1024]{2,1,0:T(8,128)}, f32[4,128,1024]{2,1,0:T(8,128)}) async-done(((f32[4,128,1024]{2,1,0:T(8,128)}, f32[4,128,1024]{2,1,0:T(8,128)}), (f32[4,128,1024]{2,1,0:T(8,128)}, f32[4,128,1024]{2,1,0:T(8,128)})) %all-reduce.3.cloned.1.call-update) | async-done | bytes 4194320 | tf_op jit(solution)/shard_map/psum | solution.py:41
  459.5 21.4 %fusion = f32[16,128,4,128]{3,1,2,0:T(8,128)S(1)} fusion(f32[4,128,1024]{2,1,0:T(8,128)} %get-tuple-element.15, f32[16,1,128,1024]{3,0,1,2:T(8,128)} %copy-done.2), kind=kOutput, calls=%fused_computation.1 | convolution fusion | flops 12884901888 | bytes 14680064 | tf_op jit(solution)/shard_map/isk,jtk->isjt/dot_general | solution.py:102
  480.9 16.4 %fusion.6 = f32[16,1,128,4,1,128]{5,2,3,0,4,1:T(8,128)S(1)} fusion(f32[16,1,128,4,1,128]{5,4,3,2,1,0:T(1,128)S(1)} %copy-done.6, f32[16,128,4,128]{3,1,2,0:T(8,128)S(1)} %fusion, pred[16,4]{1,0:T(8,128)(4,1)S(1)} %broadcast_compare_fusion, f32[4,128,1024]{2,1,0:T(8,128)S(1)} %copy-done.8, f32[16,1,128,1024]{3,2,0,1:T(8,128)} %copy-done.5), kind=kOutput, calls=%fused_computation.8 | convolution fusion | flops 12888047616 | bytes 23068736 | tf_op jit(solution)/shard_map/isk,jtk->isjt/dot_general | solution.py:99
  497.3 6.4 %copy.42 = f32[16,1,128,4,1,128]{5,4,3,2,1,0:T(1,128)} copy(f32[16,1,128,4,1,128]{5,2,3,0,4,1:T(8,128)S(1)} %fusion.6) | data formatting | bytes 8388608
  (18 shorter events, 0.0 us)
Async XLA Ops:
  7.2 76.0 %copy-start = (f32[32,1024]{1,0:T(8,128)S(1)}, f32[32,1024]{1,0:T(8,128)}, u32[]{:S(2)}) copy-start(f32[32,1024]{1,0:T(8,128)} %param.6) | copy-start | bytes 393220
  7.2 47.4 %all-gather.8.cloned.1.call-start = ((), (), s32[]{:S(2)}) async-start(), calls=%async_computation | async-start | bytes 2359296 | tf_op jit(solution)/shard_map/all_gather | solution.py:19
  14.1 64.5 %all-gather.10.cloned.1.call-start = ((), (), s32[]{:S(2)}) async-start(), calls=%async_computation.1 | async-start | bytes 6291456 | tf_op jit(solution)/shard_map/all_gather | solution.py:19
  54.6 78.1 %all-gather.12.cloned.1.call-start = ((), (), s32[]{:S(2)}) async-start(), calls=%async_computation.2 | async-start | bytes 2359296 | tf_op jit(solution)/shard_map/all_gather | solution.py:19
  81.1 2.0 copy-start.3
  81.2 51.6 %copy-start.10 = (f32[16,1,4,1024]{3,2,1,0:T(4,128)S(1)}, f32[16,1,4,1024]{3,2,1,0:T(4,128)}, u32[]{:S(2)}) copy-start(f32[16,1,4,1024]{3,2,1,0:T(4,128)} %param.7) | copy-start | bytes 786436
  81.2 51.7 %copy-start.9 = (f32[16,1,4,1024]{3,2,1,0:T(4,128)S(1)}, f32[16,1,4,1024]{3,2,1,0:T(4,128)}, u32[]{:S(2)}) copy-start(f32[16,1,4,1024]{3,2,1,0:T(4,128)} %param.8) | copy-start | bytes 786436
  94.2 62.4 %all-gather.14.cloned.1.call-start = ((), (), s32[]{:S(2)}) async-start(), calls=%async_computation.3 | async-start | bytes 6291456 | tf_op jit(solution)/shard_map/all_gather | solution.py:19
  132.7 163.4 %all-gather.16.cloned.1.call-start = ((), (), s32[]{:S(2)}) async-start(), calls=%async_computation.4 | async-start | bytes 17301504 | tf_op jit(solution)/shard_map/all_gather | solution.py:36
  140.4 319.0 %all-reduce.3.cloned.1.call-start = ((), (), s32[]{:S(2)}) async-start(), calls=%async_computation.5 | async-start | bytes 8388608 | tf_op jit(solution)/shard_map/psum | solution.py:41
  156.6 3.4 copy-start.4
  305.6 4.9 copy-start.2
  305.6 5.2 %copy-start.7 = (f32[1024,1024]{0,1:T(8,128)S(1)}, f32[1024,1024]{0,1:T(8,128)}, u32[]{:S(2)}) copy-start(f32[1024,1024]{0,1:T(8,128)} %fusion.25) | copy-start | bytes 12582916
  348.7 4.6 copy-start.5
  459.5 21.4 %copy-start.6 = (f32[16,1,128,4,1,128]{5,4,3,2,1,0:T(1,128)S(1)}, f32[16,1,128,4,1,128]{5,4,3,2,1,0:T(1,128)}, u32[]{:S(2)}) copy-start(f32[16,1,128,4,1,128]{5,4,3,2,1,0:T(1,128)} %param.9) | copy-start | bytes 12582916
  459.5 21.4 %copy-start.8 = (f32[4,128,1024]{2,1,0:T(8,128)S(1)}, f32[4,128,1024]{2,1,0:T(8,128)}, u32[]{:S(2)}) copy-start(f32[4,128,1024]{2,1,0:T(8,128)} %get-tuple-element.16) | copy-start | bytes 6291460
  480.9 22.8 %copy-start.1 = (f32[32,1024]{1,0:T(8,128)S(1)}, f32[32,1024]{1,0:T(8,128)}, u32[]{:S(2)}) copy-start(f32[32,1024]{1,0:T(8,128)} %param.6) | copy-start | bytes 393220
Sparse Core Ops, SparseCore 0:
  14.2 40.3 all-gather.7
  56.4 22.1 all-gather.9
  94.3 38.3 all-gather.11
  134.4 22.1 all-gather.13
  159.2 136.8 all-gather.15
  353.4 106.0 all-reduce.2
where the time goes:
time: 520 us; the launch traced here: 511 us
  waiting for transfers between devices  339 us (65%)
  matrix products  106 us (20%)
  local copies, waits for them, and re-layouts  33.7 us (6%)
  between operations  14.6 us (3%)
  blocking collectives  14 us (3%)
    all_gather x1, waiting for transfers between devices, in_one_piece(): lax.all_gather(both, axis, axis=dim, tiled=True)  121 us
    all_gather x4, waiting for transfers between devices, gather_in_order(): parts = lax.all_gather(parts, axes[k], axis=0, tiled=True)  119 us
    psum x1, waiting for transfers between devices, broadcast(): return lax.psum(jnp.where(mine, array, jnp.zeros_like(array)), axis)  98.7 us
    dot_general x1, matrix products, body(): jnp.dot(rows_l.reshape(-1, width), reduced, precision=exact, preferred_el...  37.9 us
    dot_general x1, matrix products, body(): jnp.einsum('isk,jtk->isjt', rows_l, col_y, precision=exact, preferred_ele...  21.4 us
    dot_general x1, matrix products, body(): jnp.einsum('isk,jtk->isjt', rows_y, col_l, precision=exact, preferred_ele...  16.4 us
    unnamed x25, local copies, waits for them, and re-layouts  16.1 us
    dot_general x1, matrix products, body(): jnp.dot(inverse_full, terms_full, precision=exact, preferred_element_type...  15.1 us
  transfers between devices with their start and end apart: 6, of which 6 were waited for; matrix products, arithmetic and copies ran while one was open for 6% of the time, Pallas kernels for 0%

commit v1 on v0

v1 whole, which is shorter than its diff:
```python
import functools

import jax
import jax.numpy as jnp
from jax import lax
from jax.experimental import pallas as pl
from jax.experimental.pallas import tpu as pltpu
from jax.sharding import PartitionSpec as P

MESH = pl.DeviceIdType.MESH
F32 = jnp.float32
BF16 = jnp.bfloat16


def comm_kernel(own, oth, eown, eoth, g_ref, cm_ref, cp_ref, h_ref,
                merged, swap, loc_sem, pre_send, pre_recv, xh_send, xh_recv,
                z_send, z_recv, d_send, d_recv, c_send, c_recv, cd_send, cd_recv,
                e_pre, ez_send, ez_recv, ey_send, ey_recv, ed_send, ed_recv):
    a = lax.axis_index("prow")
    c = lax.axis_index("pcol")
    xl, y = a // 4, a % 4
    z, xh, k = c // 4, (c // 2) % 2, c % 2
    d = c // 2

    partner = (a, c + 1 - 2 * k)
    z_next = (a, ((z + 1) % 8) * 4 + xh * 2 + k)
    z_prev = (a, ((z + 7) % 8) * 4 + xh * 2 + k)
    x_far = (a, z * 4 + (1 - xh) * 2 + k)
    x_near = ((1 - xl) * 4 + y, c)
    y_next = (xl * 4 + (y + 1) % 4, c)
    y_prev = (xl * 4 + (y + 3) % 4, c)
    z_to = (z_next, z_prev)

    def remote(src, dst, send, recv, to):
        return pltpu.make_async_remote_copy(
            src_ref=src, dst_ref=dst, send_sem=send, recv_sem=recv, device_id=to, device_id_type=MESH
        )

    barrier = pltpu.get_barrier_semaphore()
    for to in (partner, z_next, z_prev, x_far, x_near, y_next, y_prev):
        pl.semaphore_signal(barrier, inc=1, device_id=to, device_id_type=MESH)
    pl.semaphore_wait(barrier, 7)

    def h_rows(which, block, start, size):
        return h_ref.at[which, block, pl.ds(pl.multiple_of(start, 32), size), :]

    pre_e = remote(eoth, h_rows(1 - k, a, 32 * c, 32), e_pre.at[0], e_pre.at[1], partner)
    pre_e.start()
    pre = remote(oth, swap, pre_send, pre_recv, partner)
    pre.start()
    mine_e = pltpu.make_async_copy(eown, h_rows(k, a, 32 * c, 32), e_pre.at[2])
    mine_e.start()

    mine_e.wait()
    remote(eoth, h_rows(k, a, 32 * (c + 1 - 2 * k), 32), e_pre.at[0], e_pre.at[1], partner).wait_recv()
    far_e = remote(h_rows(k, a, 64 * d, 64), h_rows(k, a, 64 * d, 64), e_pre.at[3], e_pre.at[4], x_far)
    far_e.start()

    pre.wait_recv()
    merged[...] = own[...] + swap[...]

    def g_rows(which, j, n, start, size):
        return g_ref.at[which, pl.ds(j, n), :, pl.ds(pl.multiple_of(start, 8), size), :]

    far = remote(merged, g_ref.at[k, :, :, pl.ds(pl.multiple_of(8 * d, 8), 8), :], xh_send, xh_recv, x_far)
    far.start()
    mine = pltpu.make_async_copy(merged, g_ref.at[k, :, :, pl.ds(pl.multiple_of(8 * d, 8), 8), :], loc_sem)
    mine.start()

    df = 2 * z + 1 - xh
    remote(
        h_rows(k, a, 64 * df, 64), h_rows(k, a, 64 * df, 64), e_pre.at[3], e_pre.at[4], x_far
    ).wait_recv()

    def ez_copy(h, t):
        at = (z + 8 - t) % 8 if h == 0 else (z + t) % 8
        ref = h_rows(k, a, 128 * at, 128)
        return remote(ref, ref, ez_send.at[h, t], ez_recv.at[h, t], z_to[h])

    def ez_got(h, t):
        at = (z + 8 - t) % 8 if h == 0 else (z + t) % 8
        ref = h_rows(k, a, 128 * at, 128)
        return remote(ref, ref, ez_send.at[h, t - 1], ez_recv.at[h, t - 1], z_to[h])

    for h in range(2):
        ez_copy(h, 0).start()
    for t in range(1, 5):
        for h in range(2):
            if t <= (4, 3)[h]:
                ez_got(h, t).wait_recv()
                if t < (4, 3)[h]:
                    ez_copy(h, t).start()

    def plane(h, t):
        return lax.rem(z + 8 - t, 8) if h == 0 else lax.rem(z + t, 8)

    def z_ref(h, t, e):
        side = xh if e == 0 else 1 - xh
        return g_rows(k, 2 * h, 2, 16 * plane(h, t) + 8 * side, 8)

    def z_copy(h, t, e):
        ref = z_ref(h, t, e)
        return remote(ref, ref, z_send.at[h, e, t], z_recv.at[h, e, t], z_to[h])

    def z_got(h, t, e):
        ref = z_ref(h, t, e)
        return remote(ref, ref, z_send.at[h, e, t - 1], z_recv.at[h, e, t - 1], z_to[h])

    def d_copy(h, t, which=None):
        ref = g_rows(k if which is None else which, 2 * h, 2, 16 * plane(h, t), 16)
        return remote(ref, ref, d_send.at[h, t], d_recv.at[h, t], partner)

    mine.wait()
    for h in range(2):
        z_copy(h, 0, 0).start()

    def e_block(dx, dy):
        return (xl + dx) % 2 * 4 + (y + dy) % 4

    def e_copy(dx, dy, to, rdx, rdy, out):
        ref = h_ref.at[k, e_block(dx, dy)]
        return remote(ref, ref, ey_send.at[out], ey_recv.at[rdx * 4 + rdy], to)

    def e_got(dx, dy):
        ref = h_ref.at[k, e_block(dx, dy)]
        return remote(ref, ref, ey_send.at[0], ey_recv.at[dx * 4 + dy], partner)

    def e_pass(dx, dy, which=None):
        ref = h_ref.at[k if which is None else which, e_block(dx, dy)]
        return remote(ref, ref, ed_send.at[dx * 4 + dy], ed_recv.at[dx * 4 + dy], partner)

    e_sends = [
        e_copy(0, 0, x_near, 1, 0, 0),
        e_copy(0, 0, y_next, 0, 3, 1),
        e_copy(0, 0, y_prev, 0, 1, 2),
        e_copy(1, 0, y_next, 1, 3, 3),
        e_copy(1, 0, y_prev, 1, 1, 4),
        e_copy(0, 1, y_prev, 0, 2, 5),
        e_copy(1, 3, y_next, 1, 2, 6),
    ]
    for n in range(3):
        e_sends[n].start()
    e_pass(0, 0).start()

    remote(
        merged, g_ref.at[k, :, :, pl.ds(pl.multiple_of(8 * df, 8), 8), :], xh_send, xh_recv, x_far
    ).wait_recv()
    for h in range(2):
        z_copy(h, 0, 1).start()
        d_copy(h, 0).start()

    q = z // 2
    in_plane = xl == z % 2

    def place(m):
        return lax.rem(y - (2 * xh + m) + 4, 4)

    def c_ref(m, h, t):
        return cm_ref.at[m, pl.ds(2 * h, 2), pl.ds(pl.multiple_of(16 * plane(h, t), 16), 16), :]

    def c_copy(m, h, t, out, from_g):
        dst = c_ref(m, h, t)
        src = (
            g_ref.at[k, pl.ds(2 * h, 2), q, pl.ds(pl.multiple_of(16 * plane(h, t), 16), 16), :]
            if from_g
            else dst
        )
        to = (x_near, y_next, y_prev)[out]
        return remote(src, dst, c_send.at[m, h, t, out], c_recv.at[m, h, t], to)

    def cd_copy(m, h, t):
        dst = cp_ref.at[pl.ds(2 * h, 2), pl.ds(pl.multiple_of(16 * plane(h, t), 16), 16), :]
        return remote(c_ref(m, h, t), dst, cd_send.at[h, t], cd_recv.at[h, t], partner)

    def each_send(m, h, t, act):
        r = place(m)

        @pl.when(jnp.logical_and(in_plane, r == 0))
        def _():
            for out in range(3):
                act(c_copy(m, h, t, out, True))

        @pl.when(jnp.logical_and(jnp.logical_not(in_plane), r == 0))
        def _():
            for out in (1, 2):
                act(c_copy(m, h, t, out, False))

        @pl.when(r == (3 if m == 0 else 1))
        def _():
            act(c_copy(m, h, t, 2 if m == 0 else 1, False))

    def source_sends(t):
        for m in range(2):
            @pl.when(jnp.logical_and(in_plane, place(m) == 0))
            def _():
                for h in range(2):
                    for out in range(3):
                        c_copy(m, h, t, out, True).start()

    def take_columns(t, when):
        for m in range(2):
            r = place(m)
            got = jnp.logical_not(jnp.logical_and(in_plane, r == 0))
            early = jnp.logical_or(r == 0, jnp.logical_and(in_plane, r != 2))

            @pl.when(jnp.logical_and(got, early if when else jnp.logical_not(early)))
            def _():
                for h in range(2):
                    c_copy(m, h, t, 0, False).wait_recv()

                    @pl.when(r == 0)
                    def _():
                        for out in (1, 2):
                            c_copy(m, h, t, out, False).start()

                    @pl.when(r == (3 if m == 0 else 1))
                    def _():
                        c_copy(m, h, t, 2 if m == 0 else 1, False).start()

                    @pl.when(k != m)
                    def _():
                        cd_copy(m, h, t).start()

    source_sends(0)

    def step(t, carry):
        for e in range(2):
            for h in range(2):
                z_got(h, t, e).wait_recv()

                @pl.when(t < 7)
                def _():
                    z_copy(h, t, e).start()

        for h in range(2):
            d_copy(h, t).start()
        source_sends(t)
        take_columns(t - 1, True)

        @pl.when(t >= 2)
        def _():
            take_columns(t - 2, False)

        @pl.when(t == 1)
        def _():
            e_got(1, 0).wait_recv()
            e_sends[3].start()
            e_sends[4].start()
            e_pass(1, 0).start()

        @pl.when(t == 3)
        def _():
            e_got(0, 1).wait_recv()
            e_sends[5].start()
            e_pass(0, 1).start()
            e_got(0, 3).wait_recv()
            e_pass(0, 3).start()

        @pl.when(t == 4)
        def _():
            e_got(1, 3).wait_recv()
            e_sends[6].start()
            e_pass(1, 3).start()
            e_got(1, 1).wait_recv()
            e_pass(1, 1).start()

        @pl.when(t == 6)
        def _():
            for dx in range(2):
                e_got(dx, 2).wait_recv()
                e_pass(dx, 2).start()

        return carry

    lax.fori_loop(1, 8, step, 0)
    take_columns(7, True)
    take_columns(6, False)
    take_columns(7, False)

    pre_e.wait_send()
    pre.wait_send()
    far_e.wait_send()
    far.wait_send()
    for h in range(2):
        for t in range((4, 3)[h]):
            ez_copy(h, t).wait_send()
    for n in range(7):
        e_sends[n].wait_send()
    for dx in range(2):
        for dy in range(4):
            e_pass(dx, dy).wait_send()
            e_pass(dx, dy, 1 - k).wait_recv()

    def finish(t, carry):
        for h in range(2):
            @pl.when(t < 7)
            def _():
                for e in range(2):
                    z_copy(h, t, e).wait_send()

            d_copy(h, t).wait_send()
            d_copy(h, t, 1 - k).wait_recv()
            for m in range(2):
                each_send(m, h, t, lambda copy: copy.wait_send())
                source = jnp.logical_and(in_plane, place(m) == 0)

                @pl.when(jnp.logical_not(source))
                def _():
                    @pl.when(k != m)
                    def _():
                        cd_copy(m, h, t).wait_send()

                    @pl.when(k == m)
                    def _():
                        cd_copy(m, h, t).wait_recv()

        return carry

    lax.fori_loop(0, 8, finish, 0)


def gather(own, oth, eown, eoth):
    dma = pltpu.SemaphoreType.DMA
    return pl.pallas_call(
        comm_kernel,
        out_shape=(
            jax.ShapeDtypeStruct((2, 4, 4, 128, 1024), F32),
            jax.ShapeDtypeStruct((2, 4, 128, 1024), F32),
            jax.ShapeDtypeStruct((4, 128, 1024), F32),
            jax.ShapeDtypeStruct((2, 8, 1024, 128), F32),
        ),
        in_specs=[pl.BlockSpec(memory_space=pltpu.VMEM)] * 4,
        out_specs=(pl.BlockSpec(memory_space=pl.ANY),) * 4,
        scratch_shapes=[
            pltpu.VMEM((4, 4, 8, 1024), F32),
            pltpu.VMEM((4, 4, 8, 1024), F32),
            dma, dma, dma, dma, dma,
            dma((2, 2, 7)), dma((2, 2, 7)),
            dma((2, 8)), dma((2, 8)),
            dma((2, 2, 8, 3)), dma((2, 2, 8)),
            dma((2, 8)), dma((2, 8)),
            dma((5,)),
            dma((2, 4)), dma((2, 4)),
            dma((7,)), dma((8,)),
            dma((8,)), dma((8,)),
        ],
        compiler_params=pltpu.CompilerParams(collective_id=0, has_side_effects=True),
        name="gather",
    )(own, oth, eown, eoth)


def split(v):
    hi = v.astype(BF16)
    return hi, (v - hi.astype(F32)).astype(BF16)


def dot3(x, y, contract):
    (xh, xlo), (yh, ylo) = x, y
    dims = (((1,), (contract,)), ((), ()))
    dot = functools.partial(lax.dot_general, dimension_numbers=dims, preferred_element_type=F32)
    return dot(xh, yh) + dot(xlo, yh) + dot(xh, ylo)


ROWS = 608


def update_kernel(pb, fb, tr, g_ref, cm_ref, cp_ref, h_ref, pown, fown, iown,
                  red_ref, panel_ref, out_ref,
                  pc, fc, hv, ih, il, dh, dl, uh, ul, th, tl, vh, vl, sems):
    b = pl.program_id(0)
    a = lax.axis_index("prow")
    c = lax.axis_index("pcol")
    z, xh, k = c // 4, (c // 2) % 2, c % 2
    source = a == (z % 2) * 4 + 2 * xh + k

    @pl.when(b == 0)
    def _():
        load_h = pltpu.make_async_copy(h_ref, hv, sems.at[2])
        load_h.start()

        @pl.when(source)
        def _():
            pltpu.make_async_copy(g_ref.at[0, :, z // 2], pc, sems.at[0]).start()
            pltpu.make_async_copy(g_ref.at[1, :, z // 2], fc, sems.at[1]).start()

        @pl.when(jnp.logical_not(source))
        def _():
            @pl.when(k == 0)
            def _():
                pltpu.make_async_copy(cm_ref.at[0], pc, sems.at[0]).start()
                pltpu.make_async_copy(cp_ref, fc, sems.at[1]).start()

            @pl.when(k == 1)
            def _():
                pltpu.make_async_copy(cp_ref, pc, sems.at[0]).start()
                pltpu.make_async_copy(cm_ref.at[1], fc, sems.at[1]).start()

        load_h.wait()
        for g in range(8):
            lanes = slice(128 * g, 128 * g + 128)
            hi, lo = split(hv[0, g])
            ih[:, lanes] = hi
            il[:, lanes] = lo
            hi, lo = split(hv[1, g])
            dh[:, lanes] = hi
            dl[:, lanes] = lo
        pltpu.make_async_copy(cm_ref.at[0], pc, sems.at[0]).wait()
        pltpu.make_async_copy(cm_ref.at[0], fc, sems.at[1]).wait()

        hi, lo = split(fc[...].reshape(512, 1024))
        th[0:512] = hi
        tl[0:512] = lo
        hi, lo = split(fown[...])
        th[512:576] = hi
        tl[512:576] = lo
        for n in range(4):
            cols = slice(256 * n, 256 * n + 256)
            deep = slice(256 * n, 1024)
            u = dot3(
                (th[0:576, deep], tl[0:576, deep]), (ih[deep, cols], il[deep, cols]), 0
            )
            hi, lo = split(u)
            uh[0:576, cols] = hi
            ul[0:576, cols] = lo
        hi, lo = split(iown[...])
        uh[576:608] = hi
        ul[576:608] = lo
        for n in range(4):
            cols = slice(256 * n, 256 * n + 256)
            start = jnp.concatenate(
                [pc[:, :, cols].reshape(512, 256), pown[:, cols], jnp.zeros((32, 256), F32)]
            )
            t = start - dot3((uh[...], ul[...]), (dh[:, cols], dl[:, cols]), 0)
            hi, lo = split(t)
            th[:, cols] = hi
            tl[:, cols] = lo
        for n in range(4):
            cols = slice(256 * n, 256 * n + 256)
            deep = slice(0, 256 * n + 256)
            v = dot3((th[:, deep], tl[:, deep]), (ih[cols, deep], il[cols, deep]), 1)
            hi, lo = split(v[0:512])
            vh[:, cols] = hi
            vl[:, cols] = lo
            panel_ref[:, cols] = v[512:576]
            red_ref[:, cols] = -v[576:608]

    for n in range(4):
        @pl.when(b == n)
        def _():
            wide = slice(0, 128 * n + 128)
            for q in range(2):
                first = split(pb[0, 0, 2 * q:2 * q + 2].reshape(256, 1024))
                second = split(fb[0, 0, 2 * q:2 * q + 2].reshape(256, 1024))
                total = dot3(first, (uh[wide], ul[wide]), 1) + dot3(second, (vh[wide], vl[wide]), 1)
                for p in range(2):
                    i = 2 * q + p
                    lower = 8 * i + a >= c
                    for j in range(4):
                        at = pl.ds(j, 128, stride=4)
                        held = tr[i, at, :]
                        if j <= n:
                            new = held - total[128 * p:128 * p + 128, 128 * j:128 * j + 128]
                            held = jnp.where(lower, new, held) if j == n else new
                        out_ref[i, at, :] = held


def update(g, cm, cp, hh, pown, fown, iown, trailing):
    any_ = pl.BlockSpec(memory_space=pl.ANY)
    fixed = lambda shape: pl.BlockSpec(shape, lambda b: (0,) * len(shape), pipeline_mode=pl.Buffered(1))
    half = lambda which: pl.BlockSpec((1, 1, 4, 128, 1024), lambda b: (which, b, 0, 0, 0))
    tiles = pl.BlockSpec((4, 512, 128), lambda b: (b, 0, 0))
    return pl.pallas_call(
        update_kernel,
        grid=(4,),
        out_shape=(
            jax.ShapeDtypeStruct((32, 1024), F32),
            jax.ShapeDtypeStruct((64, 1024), F32),
            jax.ShapeDtypeStruct((16, 512, 128), F32),
        ),
        in_specs=[half(0), half(1), tiles, any_, any_, any_, any_,
                  fixed((64, 1024)), fixed((64, 1024)), fixed((32, 1024))],
        out_specs=(
            pl.BlockSpec((32, 1024), lambda b: (0, 0)),
            pl.BlockSpec((64, 1024), lambda b: (0, 0)),
            tiles,
        ),
        scratch_shapes=[
            pltpu.VMEM((4, 128, 1024), F32),
            pltpu.VMEM((4, 128, 1024), F32),
            pltpu.VMEM((2, 8, 1024, 128), F32),
            pltpu.VMEM((1024, 1024), BF16), pltpu.VMEM((1024, 1024), BF16),
            pltpu.VMEM((1024, 1024), BF16), pltpu.VMEM((1024, 1024), BF16),
            pltpu.VMEM((ROWS, 1024), BF16), pltpu.VMEM((ROWS, 1024), BF16),
            pltpu.VMEM((ROWS, 1024), BF16), pltpu.VMEM((ROWS, 1024), BF16),
            pltpu.VMEM((512, 1024), BF16), pltpu.VMEM((512, 1024), BF16),
            pltpu.SemaphoreType.DMA((3,)),
        ],
        compiler_params=pltpu.CompilerParams(
            dimension_semantics=("arbitrary",), vmem_limit_bytes=63 * 1024 * 1024
        ),
        name="update",
    )(g, g, trailing, g, cm, cp, hh, pown, fown, iown)


def body(inverse_factor, diag_block, panel_matrix, panel_factor, trailing):
    a = lax.axis_index("prow")
    k = lax.axis_index("pcol") % 2
    first = k == 0
    p4 = panel_matrix.reshape(4, 4, 4, 1024)
    f4 = panel_factor.reshape(4, 4, 4, 1024)

    def placed(v):
        zero = jnp.zeros_like(v)
        return jnp.concatenate([jnp.where(first, v, zero), jnp.where(first, zero, v)], axis=2)

    own = placed(jnp.where(first, p4, f4))
    oth = placed(jnp.where(first, f4, p4))
    ei = lax.dynamic_slice_in_dim(inverse_factor, 128 * a, 128, 1)
    ed = lax.dynamic_slice_in_dim(diag_block, 128 * a, 128, 1)
    g, cm, cp, hh = gather(own, oth, jnp.where(first, ei, ed), jnp.where(first, ed, ei))
    red, panel, out = update(
        g, cm, cp, hh,
        panel_matrix.reshape(64, 1024), panel_factor.reshape(64, 1024), inverse_factor,
        trailing.reshape(16, 512, 128),
    )
    return red, panel.reshape(panel_matrix.shape), out.reshape(trailing.shape)


def solution(mesh):
    rows = P(None, "prow", "pcol", None)
    tiles = P(None, "prow", None, None, "pcol", None)
    return jax.shard_map(
        body,
        mesh=mesh,
        in_specs=(P("pcol", None), P("pcol", None), rows, rows, tiles),
        out_specs=(P("pcol", None), rows, tiles),
        check_vma=False,
    )
```

time: 520 us -> 210 us (0.40); the launches traced: 511 us -> 210 us
  waiting for transfers between devices: 339 us -> 0 us
  Pallas kernels: 0 us -> 200 us
  matrix products: 106 us -> 0 us
  local copies, waits for them, and re-layouts: 33.7 us -> 5.22 us
  blocking collectives: 14 us -> 0 us
  between operations: 14.6 us -> 0.67 us
    all_gather x5 -> x0, waiting for transfers between devices: 240 us -> none  [the longest x1 121 us: in_one_piece(): lax.all_gather(both, axis, axis=dim, tiled=True)]
    pallas_call x0 -> x2, Pallas kernels: none -> 200 us  [the longest x1 170 us: gather(): pl.pallas_call(comm_kernel, out_shape=(jax.ShapeDtypeStruct((2, 4, 4, 128...]
    dot_general x7 -> x0, matrix products: 106 us -> none  [the longest x1 37.9 us: body(): jnp.dot(rows_l.reshape(-1, width), reduced, precision=exact, preferred_el...]
    psum x1 -> x0, waiting for transfers between devices: 98.7 us -> none  [broadcast(): return lax.psum(jnp.where(mine, array, jnp.zeros_like(array)), axis)]
    unnamed x25 -> x0, local copies, waits for them, and re-layouts: 16.1 us -> none
    all_gather x2 -> x0, blocking collectives: 14 us -> none  [gather_in_order(): parts = lax.all_gather(parts, axes[k], axis=0, tiled=True)]
    split x1 -> x0, local copies, waits for them, and re-layouts: 9.42 us -> none  [in_one_piece(): jnp.split(lax.all_gather(both, axis, axis=dim, tiled=True), ends, axis=al...]
    transpose x2 -> x0, local copies, waits for them, and re-layouts: 5.41 us -> none  [gather_in_order(): parts.transpose(*turned, *range(len(order), parts.ndim))]
  transfers between devices with their start and end apart: 6 -> 0, of which waited for: 6 -> 0; matrix products, arithmetic and copies ran while one was open for 6% -> 0% of each run, Pallas kernels for 0% -> 0%
where the time goes in v1:
time: 210 us
  Pallas kernels  200 us (95%)
  local copies, waits for them, and re-layouts  5.22 us (2%)
  other arithmetic  3.92 us (2%)
    pallas_call x1, Pallas kernels, gather(): pl.pallas_call(comm_kernel, out_shape=(jax.ShapeDtypeStruct((2, 4, 4, 128...  170 us
    pallas_call x1, Pallas kernels, update(): pl.pallas_call(update_kernel, grid=(4,), out_shape=(jax.ShapeDtypeStruct(...  30.7 us

profile of v1, /device:TPU:15, one launch (start us, length us, event | category | flops | bytes accessed | tf_op | source)
XLA Modules:
  0.0 210.2 jit_solution(8752950493021137176)
XLA Ops:
  0.6 1.4 dynamic-slice_select_fusion
  2.0 1.7 reshape.40.pown
  3.7 1.7 reshape.41.fown
  5.5 1.3 broadcast_select_fusion.1
  6.8 1.2 pad_maximum_fusion
  8.1 169.7 %gather.1 = (f32[2,4,4,128,1024]{4,3,2,1,0:T(8,128)}, f32[2,4,128,1024]{3,2,1,0:T(8,128)}, f32[4,128,1024]{2,1,0:T(8,128)}, f32[2,8,1024,128]{3,2,1,0:T(8,128)}) custom-call(f32[4,4,8,1024]{3,2,1,0:T(8,128)} %get-tuple-element.26.own, f32[4,4,8,1024]{3,2,1,0:T(8,128)} %get-tuple-element.27.oth, f32[32,128]{1,0:T(8,128)} %get-tuple-element.25.eown, ...), custom_call_target="tpu_custom_call" | custom-call | tf_op jit(solution)/shard_map/gather/pallas_call | solution.py:324
  177.8 30.7 %update.1 = (f32[32,1024]{1,0:T(8,128)}, f32[64,1024]{1,0:T(8,128)}, f32[16,512,128]{2,1,0:T(8,128)}) custom-call(f32[2,4,4,128,1024]{4,3,2,1,0:T(8,128)} %get-tuple-element.10.pb.fb.g_ref, f32[2,4,4,128,1024]{4,3,2,1,0:T(8,128)} %get-tuple-element.10.pb.fb.g_ref, f32[16,512,128]{2,1,0:T(8,128)} %bitcast.9, ...), custom_call_target="tpu_custom_call" | custom-call | tf_op jit(solution)/shard_map/update/pallas_call | solution.py:472
  208.5 1.7 reshape.42

commit v2 on v1

--- a/solution.py
+++ b/solution.py
@@ -44,275 +44,321 @@
     def h_rows(which, block, start, size):
         return h_ref.at[which, block, pl.ds(pl.multiple_of(start, 32), size), :]
 
+    def plane(h, t):
+        return lax.rem(z + 8 - t, 8) if h == 0 else lax.rem(z + t, 8)
+
+    def rows8(t, h, e):
+        side = xh if e == 0 else 1 - xh
+        return pl.ds(pl.multiple_of(16 * plane(h, t) + 8 * side, 8), 8)
+
     pre_e = remote(eoth, h_rows(1 - k, a, 32 * c, 32), e_pre.at[0], e_pre.at[1], partner)
     pre_e.start()
     pre = remote(oth, swap, pre_send, pre_recv, partner)
     pre.start()
     mine_e = pltpu.make_async_copy(eown, h_rows(k, a, 32 * c, 32), e_pre.at[2])
     mine_e.start()
-
     mine_e.wait()
     remote(eoth, h_rows(k, a, 32 * (c + 1 - 2 * k), 32), e_pre.at[0], e_pre.at[1], partner).wait_recv()
     far_e = remote(h_rows(k, a, 64 * d, 64), h_rows(k, a, 64 * d, 64), e_pre.at[3], e_pre.at[4], x_far)
     far_e.start()
-
     pre.wait_recv()
     merged[...] = own[...] + swap[...]
 
-    def g_rows(which, j, n, start, size):
-        return g_ref.at[which, pl.ds(j, n), :, pl.ds(pl.multiple_of(start, 8), size), :]
-
-    far = remote(merged, g_ref.at[k, :, :, pl.ds(pl.multiple_of(8 * d, 8), 8), :], xh_send, xh_recv, x_far)
-    far.start()
-    mine = pltpu.make_async_copy(merged, g_ref.at[k, :, :, pl.ds(pl.multiple_of(8 * d, 8), 8), :], loc_sem)
-    mine.start()
-
-    df = 2 * z + 1 - xh
+    def half(h):
+        return merged.at[pl.ds(2 * h, 2)]
+
+    def z_ref(h, t, e):
+        return g_ref.at[k, pl.ds(2 * h, 2), :, rows8(t, h, e), :]
+
+    for h in range(2):
+        remote(half(h), z_ref(h, 0, 0), z_send.at[h, 0, 0], z_recv.at[h, 0, 0], z_to[h]).start()
+
+    def far(h, e):
+        return remote(half(h), z_ref(h, 0, e), xh_send.at[h], xh_recv.at[h], x_far)
+
+    for h in range(2):
+        far(h, 0).start()
+    mine = [pltpu.make_async_copy(half(h), z_ref(h, 0, 0), loc_sem.at[h]) for h in range(2)]
+    for h in range(2):
+        mine[h].start()
+
+    def z_copy(h, t, e):
+        ref = z_ref(h, t, e)
+        return remote(ref, ref, z_send.at[h, e, t], z_recv.at[h, e, t], z_to[h])
+
+    def z_got(h, t, e):
+        ref = z_ref(h, t, e)
+        return remote(ref, ref, z_send.at[h, e, t - 1], z_recv.at[h, e, t - 1], z_to[h])
+
+    def d_copy(h, t, e, which=None):
+        ref = g_ref.at[k if which is None else which, pl.ds(2 * h, 2), :, rows8(t, h, e), :]
+        return remote(ref, ref, d_send.at[h, t, e], d_recv.at[h, t, e], partner)
+
+    def e_rows(which, dx, dy, h, t):
+        block = lax.rem(xl + dx, 2) * 4 + lax.rem(y + dy, 4)
+        return h_rows(which, block, 128 * plane(h, t), 128)
+
+    def ez_copy(h, t):
+        ref = e_rows(k, 0, 0, h, t)
+        return remote(ref, ref, ez_send.at[h, t], ez_recv.at[h, t], z_to[h])
+
+    def ez_got(h, t):
+        ref = e_rows(k, 0, 0, h, t)
+        return remote(ref, ref, ez_send.at[h, t - 1], ez_recv.at[h, t - 1], z_to[h])
+
+    e_hops = (
+        (0, 0, x_near, 1, 0),
+        (0, 0, y_next, 0, 3),
+        (0, 0, y_prev, 0, 1),
+        (1, 0, y_next, 1, 3),
+        (1, 0, y_prev, 1, 1),
+        (0, 1, y_prev, 0, 2),
+        (1, 3, y_next, 1, 2),
+    )
+
+    def e_copy(out, h, t):
+        dx, dy, to, rx, ry = e_hops[out]
+        ref = e_rows(k, dx, dy, h, t)
+        return remote(ref, ref, ey_send.at[out, t + 4 * h], ey_recv.at[4 * rx + ry, t + 4 * h], to)
+
+    def e_got(dx, dy, h, t):
+        ref = e_rows(k, dx, dy, h, t)
+        return remote(ref, ref, ey_send.at[0, t + 4 * h], ey_recv.at[4 * dx + dy, t + 4 * h], partner)
+
+    def e_pass(dx, dy, which=None):
+        block = lax.rem(xl + dx, 2) * 4 + lax.rem(y + dy, 4)
+        ref = h_ref.at[k if which is None else which, block]
+        return remote(ref, ref, ed_send.at[4 * dx + dy], ed_recv.at[4 * dx + dy], partner)
+
+    def valid(h, t):
+        return jnp.logical_and(t >= h, t <= 4 - h)
+
+    def e_step(s):
+        for h in range(2):
+            @pl.when(s <= 4 - h)
+            def _():
+                ez_got(h, s).wait_recv()
+
+                @pl.when(s < 4 - h)
+                def _():
+                    ez_copy(h, s).start()
+
+                for out in range(3):
+                    e_copy(out, h, s).start()
+
+            @pl.when(valid(h, s - 1))
+            def _():
+                t = jnp.maximum(s - 1, h)
+                e_got(1, 0, h, t).wait_recv()
+                e_copy(3, h, t).start()
+                e_copy(4, h, t).start()
+                e_got(0, 1, h, t).wait_recv()
+                e_copy(5, h, t).start()
+                e_got(0, 3, h, t).wait_recv()
+
+            @pl.when(valid(h, s - 2))
+            def _():
+                t = jnp.maximum(s - 2, h)
+                e_got(1, 3, h, t).wait_recv()
+                e_copy(6, h, t).start()
+                e_got(1, 1, h, t).wait_recv()
+
+            @pl.when(valid(h, s - 3))
+            def _():
+                t = jnp.maximum(s - 3, h)
+                e_got(0, 2, h, t).wait_recv()
+                e_got(1, 2, h, t).wait_recv()
+
+        @pl.when(s == 4)
+        def _():
+            e_pass(0, 0).start()
+
+        @pl.when(s == 5)
+        def _():
+            for dx, dy in ((1, 0), (0, 1), (0, 3)):
+                e_pass(dx, dy).start()
+
+        @pl.when(s == 6)
+        def _():
+            for dx, dy in ((1, 3), (1, 1)):
+                e_pass(dx, dy).start()
+
+        @pl.when(s == 7)
+        def _():
+            for dx, dy in ((0, 2), (1, 2)):
+                e_pass(dx, dy).start()
+
+    q = z // 2
+    in_plane = xl == z % 2
+    y_out = (2, 1)
+
+    def place(m):
+        return lax.rem(y - (2 * xh + m) + 4, 4)
+
+    def c_copy(m, h, t, e, out, from_g=False):
+        dst = cm_ref.at[m, pl.ds(2 * h, 2), rows8(t, h, e), :]
+        src = g_ref.at[k, pl.ds(2 * h, 2), q, rows8(t, h, e), :] if from_g else dst
+        to = (x_near, y_next, y_prev)[out]
+        return remote(src, dst, c_send.at[m, h, t, e, out], c_recv.at[m, h, t, e], to)
+
+    def cd_copy(m, h, t, e):
+        src = cm_ref.at[m, pl.ds(2 * h, 2), rows8(t, h, e), :]
+        dst = cp_ref.at[pl.ds(2 * h, 2), rows8(t, h, e), :]
+        return remote(src, dst, cd_send.at[h, t, e], cd_recv.at[h, t, e], partner)
+
+    def is_source(m):
+        return jnp.logical_and(in_plane, place(m) == 0)
+
+    def off_root(m):
+        return jnp.logical_and(jnp.logical_not(in_plane), place(m) == 0)
+
+    def relays(m):
+        return place(m) == (3, 1)[m]
+
+    def source_sends(t, e):
+        for m in range(2):
+            @pl.when(is_source(m))
+            def _():
+                for h in range(2):
+                    for out in range(3):
+                        c_copy(m, h, t, e, out, True).start()
+
+    def take_columns(t, e, lag):
+        for m in range(2):
+            r = place(m)
+            when = (
+                jnp.logical_or(off_root(m), jnp.logical_and(in_plane, r % 2 == 1)),
+                jnp.logical_or(
+                    jnp.logical_and(in_plane, r == 2),
+                    jnp.logical_and(jnp.logical_not(in_plane), r % 2 == 1),
+                ),
+                jnp.logical_and(jnp.logical_not(in_plane), r == 2),
+            )[lag - 1]
+
+            @pl.when(jnp.logical_and(when, t >= 0))
+            def _():
+                s = jnp.maximum(t, 0)
+                for h in range(2):
+                    c_copy(m, h, s, e, 0).wait_recv()
+
+                    @pl.when(r == 0)
+                    def _():
+                        for out in (1, 2):
+                            c_copy(m, h, s, e, out).start()
+
+                    @pl.when(relays(m))
+                    def _():
+                        c_copy(m, h, s, e, y_out[m]).start()
+
+                    @pl.when(k != m)
+                    def _():
+                        cd_copy(m, h, s, e).start()
+
+    def after(t, e):
+        for h in range(2):
+            d_copy(h, t, e).start()
+        source_sends(t, e)
+
+    mine[0].wait()
+    mine[1].wait()
+    df = d + 1 - 2 * xh
     remote(
         h_rows(k, a, 64 * df, 64), h_rows(k, a, 64 * df, 64), e_pre.at[3], e_pre.at[4], x_far
     ).wait_recv()
-
-    def ez_copy(h, t):
-        at = (z + 8 - t) % 8 if h == 0 else (z + t) % 8
-        ref = h_rows(k, a, 128 * at, 128)
-        return remote(ref, ref, ez_send.at[h, t], ez_recv.at[h, t], z_to[h])
-
-    def ez_got(h, t):
-        at = (z + 8 - t) % 8 if h == 0 else (z + t) % 8
-        ref = h_rows(k, a, 128 * at, 128)
-        return remote(ref, ref, ez_send.at[h, t - 1], ez_recv.at[h, t - 1], z_to[h])
-
     for h in range(2):
         ez_copy(h, 0).start()
-    for t in range(1, 5):
+    for out in range(3):
+        e_copy(out, 0, 0).start()
+    after(0, 0)
+
+    def step(s, carry):
         for h in range(2):
-            if t <= (4, 3)[h]:
-                ez_got(h, t).wait_recv()
-                if t < (4, 3)[h]:
-                    ez_copy(h, t).start()
-
-    def plane(h, t):
-        return lax.rem(z + 8 - t, 8) if h == 0 else lax.rem(z + t, 8)
-
-    def z_ref(h, t, e):
-        side = xh if e == 0 else 1 - xh
-        return g_rows(k, 2 * h, 2, 16 * plane(h, t) + 8 * side, 8)
-
-    def z_copy(h, t, e):
-        ref = z_ref(h, t, e)
-        return remote(ref, ref, z_send.at[h, e, t], z_recv.at[h, e, t], z_to[h])
-
-    def z_got(h, t, e):
-        ref = z_ref(h, t, e)
-        return remote(ref, ref, z_send.at[h, e, t - 1], z_recv.at[h, e, t - 1], z_to[h])
-
-    def d_copy(h, t, which=None):
-        ref = g_rows(k if which is None else which, 2 * h, 2, 16 * plane(h, t), 16)
-        return remote(ref, ref, d_send.at[h, t], d_recv.at[h, t], partner)
-
-    mine.wait()
+            z_got(h, s, 0).wait_recv()
+
+            @pl.when(s < 7)
+            def _():
+                z_copy(h, s, 0).start()
+
+        after(s, 0)
+        for lag in (1, 2, 3):
+            take_columns(s - lag, 0, lag)
+        e_step(s)
+        t = s - 1
+        for h in range(2):
+            @pl.when(t == 0)
+            def _():
+                far(h, 1).wait_recv()
+
+            @pl.when(t > 0)
+            def _():
+                z_got(h, jnp.maximum(t, 1), 1).wait_recv()
+
+            z_copy(h, t, 1).start()
+
+        after(t, 1)
+        for lag in (1, 2, 3):
+            take_columns(t - lag, 1, lag)
+        return carry
+
+    lax.fori_loop(1, 8, step, 0)
+    last = jnp.int32(7)
     for h in range(2):
-        z_copy(h, 0, 0).start()
-
-    def e_block(dx, dy):
-        return (xl + dx) % 2 * 4 + (y + dy) % 4
-
-    def e_copy(dx, dy, to, rdx, rdy, out):
-        ref = h_ref.at[k, e_block(dx, dy)]
-        return remote(ref, ref, ey_send.at[out], ey_recv.at[rdx * 4 + rdy], to)
-
-    def e_got(dx, dy):
-        ref = h_ref.at[k, e_block(dx, dy)]
-        return remote(ref, ref, ey_send.at[0], ey_recv.at[dx * 4 + dy], partner)
-
-    def e_pass(dx, dy, which=None):
-        ref = h_ref.at[k if which is None else which, e_block(dx, dy)]
-        return remote(ref, ref, ed_send.at[dx * 4 + dy], ed_recv.at[dx * 4 + dy], partner)
-
-    e_sends = [
-        e_copy(0, 0, x_near, 1, 0, 0),
-        e_copy(0, 0, y_next, 0, 3, 1),
-        e_copy(0, 0, y_prev, 0, 1, 2),
-        e_copy(1, 0, y_next, 1, 3, 3),
-        e_copy(1, 0, y_prev, 1, 1, 4),
-        e_copy(0, 1, y_prev, 0, 2, 5),
-        e_copy(1, 3, y_next, 1, 2, 6),
-    ]
-    for n in range(3):
-        e_sends[n].start()
-    e_pass(0, 0).start()
-
-    remote(
-        merged, g_ref.at[k, :, :, pl.ds(pl.multiple_of(8 * df, 8), 8), :], xh_send, xh_recv, x_far
-    ).wait_recv()
-    for h in range(2):
-        z_copy(h, 0, 1).start()
-        d_copy(h, 0).start()
-
-    q = z // 2
-    in_plane = xl == z % 2
-
-    def place(m):
-        return lax.rem(y - (2 * xh + m) + 4, 4)
-
-    def c_ref(m, h, t):
-        return cm_ref.at[m, pl.ds(2 * h, 2), pl.ds(pl.multiple_of(16 * plane(h, t), 16), 16), :]
-
-    def c_copy(m, h, t, out, from_g):
-        dst = c_ref(m, h, t)
-        src = (
-            g_ref.at[k, pl.ds(2 * h, 2), q, pl.ds(pl.multiple_of(16 * plane(h, t), 16), 16), :]
-            if from_g
-            else dst
-        )
-        to = (x_near, y_next, y_prev)[out]
-        return remote(src, dst, c_send.at[m, h, t, out], c_recv.at[m, h, t], to)
-
-    def cd_copy(m, h, t):
-        dst = cp_ref.at[pl.ds(2 * h, 2), pl.ds(pl.multiple_of(16 * plane(h, t), 16), 16), :]
-        return remote(c_ref(m, h, t), dst, cd_send.at[h, t], cd_recv.at[h, t], partner)
-
-    def each_send(m, h, t, act):
-        r = place(m)
-
-        @pl.when(jnp.logical_and(in_plane, r == 0))
-        def _():
-            for out in range(3):
-                act(c_copy(m, h, t, out, True))
-
-        @pl.when(jnp.logical_and(jnp.logical_not(in_plane), r == 0))
-        def _():
-            for out in (1, 2):
-                act(c_copy(m, h, t, out, False))
-
-        @pl.when(r == (3 if m == 0 else 1))
-        def _():
-            act(c_copy(m, h, t, 2 if m == 0 else 1, False))
-
-    def source_sends(t):
-        for m in range(2):
-            @pl.when(jnp.logical_and(in_plane, place(m) == 0))
-            def _():
-                for h in range(2):
-                    for out in range(3):
-                        c_copy(m, h, t, out, True).start()
-
-    def take_columns(t, when):
-        for m in range(2):
-            r = place(m)
-            got = jnp.logical_not(jnp.logical_and(in_plane, r == 0))
-            early = jnp.logical_or(r == 0, jnp.logical_and(in_plane, r != 2))
-
-            @pl.when(jnp.logical_and(got, early if when else jnp.logical_not(early)))
-            def _():
-                for h in range(2):
-                    c_copy(m, h, t, 0, False).wait_recv()
-
-                    @pl.when(r == 0)
-                    def _():
-                        for out in (1, 2):
-                            c_copy(m, h, t, out, False).start()
-
-                    @pl.when(r == (3 if m == 0 else 1))
-                    def _():
-                        c_copy(m, h, t, 2 if m == 0 else 1, False).start()
-
-                    @pl.when(k != m)
-                    def _():
-                        cd_copy(m, h, t).start()
-
-    source_sends(0)
-
-    def step(t, carry):
-        for e in range(2):
-            for h in range(2):
-                z_got(h, t, e).wait_recv()
-
-                @pl.when(t < 7)
-                def _():
-                    z_copy(h, t, e).start()
-
-        for h in range(2):
-            d_copy(h, t).start()
-        source_sends(t)
-        take_columns(t - 1, True)
-
-        @pl.when(t >= 2)
-        def _():
-            take_columns(t - 2, False)
-
-        @pl.when(t == 1)
-        def _():
-            e_got(1, 0).wait_recv()
-            e_sends[3].start()
-            e_sends[4].start()
-            e_pass(1, 0).start()
-
-        @pl.when(t == 3)
-        def _():
-            e_got(0, 1).wait_recv()
-            e_sends[5].start()
-            e_pass(0, 1).start()
-            e_got(0, 3).wait_recv()
-            e_pass(0, 3).start()
-
-        @pl.when(t == 4)
-        def _():
-            e_got(1, 3).wait_recv()
-            e_sends[6].start()
-            e_pass(1, 3).start()
-            e_got(1, 1).wait_recv()
-            e_pass(1, 1).start()
-
-        @pl.when(t == 6)
-        def _():
-            for dx in range(2):
-                e_got(dx, 2).wait_recv()
-                e_pass(dx, 2).start()
-
-        return carry
-
-    lax.fori_loop(1, 8, step, 0)
-    take_columns(7, True)
-    take_columns(6, False)
-    take_columns(7, False)
+        z_got(h, last, 1).wait_recv()
+    after(last, 1)
+    for lag in (1, 2, 3):
+        for back in range(lag, -1, -1):
+            if back < lag:
+                take_columns(last - back, 0, lag)
+            take_columns(last - back, 1, lag)
 
     pre_e.wait_send()
     pre.wait_send()
     far_e.wait_send()
-    far.wait_send()
     for h in range(2):
-        for t in range((4, 3)[h]):
+        far(h, 0).wait_send()
+        for t in range(4 - h):
             ez_copy(h, t).wait_send()
-    for n in range(7):
-        e_sends[n].wait_send()
+        for t in range(h, 5 - h):
+            for out in range(7):
+                e_copy(out, h, t).wait_send()
     for dx in range(2):
         for dy in range(4):
             e_pass(dx, dy).wait_send()
             e_pass(dx, dy, 1 - k).wait_recv()
 
     def finish(t, carry):
-        for h in range(2):
-            @pl.when(t < 7)
-            def _():
-                for e in range(2):
+        for e in range(2):
+            for h in range(2):
+                @pl.when(t < 7)
+                def _():
                     z_copy(h, t, e).wait_send()
 
-            d_copy(h, t).wait_send()
-            d_copy(h, t, 1 - k).wait_recv()
-            for m in range(2):
-                each_send(m, h, t, lambda copy: copy.wait_send())
-                source = jnp.logical_and(in_plane, place(m) == 0)
-
-                @pl.when(jnp.logical_not(source))
-                def _():
-                    @pl.when(k != m)
-                    def _():
-                        cd_copy(m, h, t).wait_send()
-
-                    @pl.when(k == m)
-                    def _():
-                        cd_copy(m, h, t).wait_recv()
+                d_copy(h, t, e).wait_send()
+                d_copy(h, t, e, 1 - k).wait_recv()
+                for m in range(2):
+                    @pl.when(is_source(m))
+                    def _():
+                        for out in range(3):
+                            c_copy(m, h, t, e, out, True).wait_send()
+
+                    @pl.when(off_root(m))
+                    def _():
+                        for out in (1, 2):
+                            c_copy(m, h, t, e, out).wait_send()
+
+                    @pl.when(relays(m))
+                    def _():
+                        c_copy(m, h, t, e, y_out[m]).wait_send()
+
+                    @pl.when(jnp.logical_not(is_source(m)))
+                    def _():
+                        @pl.when(k != m)
+                        def _():
+                            cd_copy(m, h, t, e).wait_send()
+
+                        @pl.when(k == m)
+                        def _():
+                            cd_copy(m, h, t, e).wait_recv()
 
         return carry
 
@@ -334,14 +380,14 @@
         scratch_shapes=[
             pltpu.VMEM((4, 4, 8, 1024), F32),
             pltpu.VMEM((4, 4, 8, 1024), F32),
-            dma, dma, dma, dma, dma,
+            dma((2,)), dma, dma, dma((2,)), dma((2,)),
             dma((2, 2, 7)), dma((2, 2, 7)),
-            dma((2, 8)), dma((2, 8)),
-            dma((2, 2, 8, 3)), dma((2, 2, 8)),
-            dma((2, 8)), dma((2, 8)),
+            dma((2, 8, 2)), dma((2, 8, 2)),
+            dma((2, 2, 8, 2, 3)), dma((2, 2, 8, 2)),
+            dma((2, 8, 2)), dma((2, 8, 2)),
             dma((5,)),
             dma((2, 4)), dma((2, 4)),
-            dma((7,)), dma((8,)),
+            dma((7, 8)), dma((8, 8)),
             dma((8,)), dma((8,)),
         ],
         compiler_params=pltpu.CompilerParams(collective_id=0, has_side_effects=True),

time: 210 us -> 165 us (0.79)
  Pallas kernels: 200 us -> 154 us
    pallas_call x1, Pallas kernels: 170 us -> 124 us  [gather(): pl.pallas_call(comm_kernel, out_shape=(jax.ShapeDtypeStruct((2, 4, 4, 128...]
where the time goes in v2:
time: 165 us; the launch traced here: 164 us
  Pallas kernels  154 us (93%)
  local copies, waits for them, and re-layouts  5.22 us (3%)
  other arithmetic  3.92 us (2%)
    pallas_call x1, Pallas kernels, gather(): pl.pallas_call(comm_kernel, out_shape=(jax.ShapeDtypeStruct((2, 4, 4, 128...  124 us
    pallas_call x1, Pallas kernels, update(): pl.pallas_call(update_kernel, grid=(4,), out_shape=(jax.ShapeDtypeStruct(...  30.7 us

profile of v2, /device:TPU:15, one launch (start us, length us, event | category | flops | bytes accessed | tf_op | source)
XLA Modules:
  0.0 164.2 jit_solution(18150476544861169498)
XLA Ops:
  0.6 1.4 dynamic-slice_select_fusion
  2.0 1.7 %reshape.40.pown = f32[64,1024]{1,0:T(8,128)} reshape(f32[16,1,4,1024]{3,2,1,0:T(4,128)} %param.7) | data formatting | bytes 524288 | tf_op jit(solution)/shard_map/reshape | solution.py:569
  3.7 1.7 %reshape.41.fown = f32[64,1024]{1,0:T(8,128)} reshape(f32[16,1,4,1024]{3,2,1,0:T(4,128)} %param.8) | data formatting | bytes 524288 | tf_op jit(solution)/shard_map/reshape | solution.py:569
  5.5 1.3 broadcast_select_fusion.1
  6.8 1.2 pad_maximum_fusion
  8.1 123.8 %gather.1 = (f32[2,4,4,128,1024]{4,3,2,1,0:T(8,128)}, f32[2,4,128,1024]{3,2,1,0:T(8,128)}, f32[4,128,1024]{2,1,0:T(8,128)}, f32[2,8,1024,128]{3,2,1,0:T(8,128)}) custom-call(f32[4,4,8,1024]{3,2,1,0:T(8,128)} %get-tuple-element.26.own, f32[4,4,8,1024]{3,2,1,0:T(8,128)} %get-tuple-element.27.oth, f32[32,128]{1,0:T(8,128)} %get-tuple-element.25.eown, ...), custom_call_target="tpu_custom_call" | custom-call | tf_op jit(solution)/shard_map/gather/pallas_call | solution.py:370
  131.8 30.7 %update.1 = (f32[32,1024]{1,0:T(8,128)}, f32[64,1024]{1,0:T(8,128)}, f32[16,512,128]{2,1,0:T(8,128)}) custom-call(f32[2,4,4,128,1024]{4,3,2,1,0:T(8,128)} %get-tuple-element.10.pb.fb.g_ref, f32[2,4,4,128,1024]{4,3,2,1,0:T(8,128)} %get-tuple-element.10.pb.fb.g_ref, f32[16,512,128]{2,1,0:T(8,128)} %bitcast.9, ...), custom_call_target="tpu_custom_call" | custom-call | tf_op jit(solution)/shard_map/update/pallas_call | solution.py:518
  162.5 1.7 %reshape.42 = f32[16,1,4,1024]{3,2,0,1:T(4,128)} reshape(f32[64,1024]{1,0:T(8,128)} %get-tuple-element.15) | data formatting | bytes 524288 | tf_op jit(solution)/shard_map/reshape | solution.py:572

commit v3 on v2

--- a/solution.py
+++ b/solution.py
@@ -12,10 +12,18 @@
 BF16 = jnp.bfloat16
 
 
-def comm_kernel(own, oth, eown, eoth, g_ref, cm_ref, cp_ref, h_ref,
+E_PASSES = (
+    (4, ((0, 0),)),
+    (5, ((1, 0), (0, 1), (0, 3))),
+    (6, ((1, 3), (1, 1))),
+    (7, ((0, 2), (1, 2))),
+)
+
+
+def comm_kernel(p_ref, f_ref, inv_ref, diag_ref, g_ref, cm_ref, cp_ref, h_ref,
                 merged, swap, loc_sem, pre_send, pre_recv, xh_send, xh_recv,
-                z_send, z_recv, d_send, d_recv, c_send, c_recv, cd_send, cd_recv,
-                e_pre, ez_send, ez_recv, ey_send, ey_recv, ed_send, ed_recv):
+                z_send, z_recv, d_send, d_recv, c_send, c_recv, cf_send, cd_send, cd_recv,
+                xf_send, xf_recv, e_pre, ez_send, ez_recv, ey_send, ey_recv, ed_send, ed_recv):
     a = lax.axis_index("prow")
     c = lax.axis_index("pcol")
     xl, y = a // 4, a % 4
@@ -27,6 +35,7 @@
     z_prev = (a, ((z + 7) % 8) * 4 + xh * 2 + k)
     x_far = (a, z * 4 + (1 - xh) * 2 + k)
     x_near = ((1 - xl) * 4 + y, c)
+    x_side = ((1 - xl) * 4 + y, z * 4 + (1 - xh) * 2 + k)
     y_next = (xl * 4 + (y + 1) % 4, c)
     y_prev = (xl * 4 + (y + 3) % 4, c)
     z_to = (z_next, z_prev)
@@ -37,9 +46,9 @@
         )
 
     barrier = pltpu.get_barrier_semaphore()
-    for to in (partner, z_next, z_prev, x_far, x_near, y_next, y_prev):
+    for to in (partner, z_next, z_prev, x_far, x_near, x_side, y_next, y_prev):
         pl.semaphore_signal(barrier, inc=1, device_id=to, device_id_type=MESH)
-    pl.semaphore_wait(barrier, 7)
+    pl.semaphore_wait(barrier, 8)
 
     def h_rows(which, block, start, size):
         return h_ref.at[which, block, pl.ds(pl.multiple_of(start, 32), size), :]
@@ -48,33 +57,50 @@
         return lax.rem(z + 8 - t, 8) if h == 0 else lax.rem(z + t, 8)
 
     def rows8(t, h, e):
-        side = xh if e == 0 else 1 - xh
+        side = lax.rem(xh + e, 2)
         return pl.ds(pl.multiple_of(16 * plane(h, t) + 8 * side, 8), 8)
 
-    pre_e = remote(eoth, h_rows(1 - k, a, 32 * c, 32), e_pre.at[0], e_pre.at[1], partner)
-    pre_e.start()
-    pre = remote(oth, swap, pre_send, pre_recv, partner)
-    pre.start()
-    mine_e = pltpu.make_async_copy(eown, h_rows(k, a, 32 * c, 32), e_pre.at[2])
-    mine_e.start()
+    lanes = pl.ds(pl.multiple_of(128 * a, 128), 128)
+    pairs = ((p_ref, f_ref, inv_ref, diag_ref), (f_ref, p_ref, diag_ref, inv_ref))
+    for me in range(2):
+        @pl.when(k == me)
+        def _():
+            _, other, e_own, e_other = pairs[me]
+            remote(
+                e_other.at[:, lanes], h_rows(1 - me, a, 32 * c, 32), e_pre.at[0], e_pre.at[1], partner
+            ).start()
+            remote(other, swap, pre_send, pre_recv, partner).start()
+            pltpu.make_async_copy(e_own.at[:, lanes], h_rows(me, a, 32 * c, 32), e_pre.at[2]).start()
+
+    pre = remote(f_ref, swap, pre_send, pre_recv, partner)
+    mine_e = pltpu.make_async_copy(inv_ref.at[:, lanes], h_rows(k, a, 32 * c, 32), e_pre.at[2])
     mine_e.wait()
-    remote(eoth, h_rows(k, a, 32 * (c + 1 - 2 * k), 32), e_pre.at[0], e_pre.at[1], partner).wait_recv()
+    pre_e = remote(
+        inv_ref.at[:, lanes], h_rows(k, a, 32 * (c + 1 - 2 * k), 32), e_pre.at[0], e_pre.at[1], partner
+    )
+    pre_e.wait_recv()
     far_e = remote(h_rows(k, a, 64 * d, 64), h_rows(k, a, 64 * d, 64), e_pre.at[3], e_pre.at[4], x_far)
     far_e.start()
     pre.wait_recv()
-    merged[...] = own[...] + swap[...]
+    merged[:, :, 0:4, :] = jnp.where(k == 0, p_ref[...], swap[...])
+    merged[:, :, 4:8, :] = jnp.where(k == 0, swap[...], f_ref[...])
 
     def half(h):
         return merged.at[pl.ds(2 * h, 2)]
 
     def z_ref(h, t, e):
-        return g_ref.at[k, pl.ds(2 * h, 2), :, rows8(t, h, e), :]
+        return g_ref.at[k, pl.ds(2 * h, 2), pl.ds(0, 4 - e), rows8(t, h, e), :]
 
     for h in range(2):
         remote(half(h), z_ref(h, 0, 0), z_send.at[h, 0, 0], z_recv.at[h, 0, 0], z_to[h]).start()
 
     def far(h, e):
-        return remote(half(h), z_ref(h, 0, e), xh_send.at[h], xh_recv.at[h], x_far)
+        ref = g_ref.at[k, pl.ds(2 * h, 2), :, rows8(0, h, e), :]
+        return remote(half(h), ref, xh_send.at[h], xh_recv.at[h], x_far)
+
+    def xf_copy(h, t, e):
+        ref = g_ref.at[k, pl.ds(2 * h, 2), pl.ds(3, 1), rows8(t, h, e), :]
+        return remote(ref, ref, xf_send.at[h, t], xf_recv.at[h, t], x_far)
 
     for h in range(2):
         far(h, 0).start()
@@ -125,17 +151,27 @@
         ref = e_rows(k, dx, dy, h, t)
         return remote(ref, ref, ey_send.at[0, t + 4 * h], ey_recv.at[4 * dx + dy, t + 4 * h], partner)
 
-    def e_pass(dx, dy, which=None):
-        block = lax.rem(xl + dx, 2) * 4 + lax.rem(y + dy, 4)
-        ref = h_ref.at[k if which is None else which, block]
-        return remote(ref, ref, ed_send.at[4 * dx + dy], ed_recv.at[4 * dx + dy], partner)
+    def blk(dx, dy):
+        return lax.rem(xl + dx, 2) * 4 + lax.rem(y + dy, 4)
+
+    def lower(dx, dy, h, t):
+        return plane(h, t) >= blk(dx, dy)
 
     def valid(h, t):
         return jnp.logical_and(t >= h, t <= 4 - h)
 
+    def e_take(out_got, outs, h, t):
+        dx, dy = out_got
+
+        @pl.when(lower(dx, dy, h, t))
+        def _():
+            e_got(dx, dy, h, t).wait_recv()
+            for out in outs:
+                e_copy(out, h, t).start()
+
     def e_step(s):
         for h in range(2):
-            @pl.when(s <= 4 - h)
+            @pl.when(jnp.logical_and(s <= 4 - h, lower(0, 0, h, s)))
             def _():
                 ez_got(h, s).wait_recv()
 
@@ -149,44 +185,41 @@
             @pl.when(valid(h, s - 1))
             def _():
                 t = jnp.maximum(s - 1, h)
-                e_got(1, 0, h, t).wait_recv()
-                e_copy(3, h, t).start()
-                e_copy(4, h, t).start()
-                e_got(0, 1, h, t).wait_recv()
-                e_copy(5, h, t).start()
-                e_got(0, 3, h, t).wait_recv()
+                e_take((1, 0), (3, 4), h, t)
+                e_take((0, 1), (5,), h, t)
+                e_take((0, 3), (), h, t)
 
             @pl.when(valid(h, s - 2))
             def _():
                 t = jnp.maximum(s - 2, h)
-                e_got(1, 3, h, t).wait_recv()
-                e_copy(6, h, t).start()
-                e_got(1, 1, h, t).wait_recv()
+                e_take((1, 3), (6,), h, t)
+                e_take((1, 1), (), h, t)
 
             @pl.when(valid(h, s - 3))
             def _():
                 t = jnp.maximum(s - 3, h)
-                e_got(0, 2, h, t).wait_recv()
-                e_got(1, 2, h, t).wait_recv()
-
-        @pl.when(s == 4)
-        def _():
-            e_pass(0, 0).start()
-
-        @pl.when(s == 5)
-        def _():
-            for dx, dy in ((1, 0), (0, 1), (0, 3)):
-                e_pass(dx, dy).start()
-
-        @pl.when(s == 6)
-        def _():
-            for dx, dy in ((1, 3), (1, 1)):
-                e_pass(dx, dy).start()
-
-        @pl.when(s == 7)
-        def _():
-            for dx, dy in ((0, 2), (1, 2)):
-                e_pass(dx, dy).start()
+                e_take((0, 2), (), h, t)
+                e_take((1, 2), (), h, t)
+
+        for at, blocks in E_PASSES:
+            @pl.when(s == at)
+            def _():
+                e_pass_all(blocks, lambda copy: copy.start())
+
+    def e_piece(dx, dy, p, which):
+        ref = h_rows(which, blk(dx, dy), 128 * p, 128)
+        return remote(ref, ref, ed_send.at[4 * dx + dy, p], ed_recv.at[4 * dx + dy, p], partner)
+
+    def e_pass_all(blocks, act, which=None):
+        def piece(p, carry):
+            for dx, dy in blocks:
+                @pl.when(p >= blk(dx, dy))
+                def _():
+                    act(e_piece(dx, dy, p, k if which is None else which))
+
+            return carry
+
+        lax.fori_loop(0, 8, piece, 0)
 
     q = z // 2
     in_plane = xl == z % 2
@@ -215,15 +248,27 @@
     def relays(m):
         return place(m) == (3, 1)[m]
 
+    def is_side(m):
+        return jnp.logical_and(in_plane, y == 2 * (1 - xh) + m)
+
+    def side_copy(m, t, e):
+        src = g_ref.at[k, pl.ds(2, 2), q, rows8(t, 1, e), :]
+        dst = cm_ref.at[m, pl.ds(2, 2), rows8(t, 1, e), :]
+        return remote(src, dst, cf_send.at[m, t, e], c_recv.at[m, 1, t, 1 - e], x_side)
+
     def source_sends(t, e):
         for m in range(2):
             @pl.when(is_source(m))
             def _():
                 for h in range(2):
-                    for out in range(3):
+                    for out in range(h, 3):
                         c_copy(m, h, t, e, out, True).start()
 
-    def take_columns(t, e, lag):
+            @pl.when(is_side(m))
+            def _():
+                side_copy(m, t, e).start()
+
+    def take_columns(t, slot, lag):
         for m in range(2):
             r = place(m)
             when = (
@@ -239,6 +284,7 @@
             def _():
                 s = jnp.maximum(t, 0)
                 for h in range(2):
+                    e = jnp.where(in_plane, slot, 1 - slot) if h == 1 else slot
                     c_copy(m, h, s, e, 0).wait_recv()
 
                     @pl.when(r == 0)
@@ -265,10 +311,13 @@
     remote(
         h_rows(k, a, 64 * df, 64), h_rows(k, a, 64 * df, 64), e_pre.at[3], e_pre.at[4], x_far
     ).wait_recv()
-    for h in range(2):
-        ez_copy(h, 0).start()
-    for out in range(3):
-        e_copy(out, 0, 0).start()
+    @pl.when(lower(0, 0, 0, 0))
+    def _():
+        for h in range(2):
+            ez_copy(h, 0).start()
+        for out in range(3):
+            e_copy(out, 0, 0).start()
+
     after(0, 0)
 
     def step(s, carry):
@@ -278,6 +327,8 @@
             @pl.when(s < 7)
             def _():
                 z_copy(h, s, 0).start()
+
+            xf_copy(h, s, 0).start()
 
         after(s, 0)
         for lag in (1, 2, 3):
@@ -295,6 +346,11 @@
 
             z_copy(h, t, 1).start()
 
+        for h in range(2):
+            @pl.when(t > 0)
+            def _():
+                xf_copy(h, t, 1).wait_recv()
+
         after(t, 1)
         for lag in (1, 2, 3):
             take_columns(t - lag, 1, lag)
@@ -304,6 +360,7 @@
     last = jnp.int32(7)
     for h in range(2):
         z_got(h, last, 1).wait_recv()
+        xf_copy(h, last, 1).wait_recv()
     after(last, 1)
     for lag in (1, 2, 3):
         for back in range(lag, -1, -1):
@@ -316,15 +373,21 @@
     far_e.wait_send()
     for h in range(2):
         far(h, 0).wait_send()
-        for t in range(4 - h):
-            ez_copy(h, t).wait_send()
-        for t in range(h, 5 - h):
-            for out in range(7):
-                e_copy(out, h, t).wait_send()
-    for dx in range(2):
-        for dy in range(4):
-            e_pass(dx, dy).wait_send()
-            e_pass(dx, dy, 1 - k).wait_recv()
+        for t in range(5 - h):
+            if t < 4 - h:
+                @pl.when(lower(0, 0, h, t))
+                def _():
+                    ez_copy(h, t).wait_send()
+
+            if t >= h:
+                for out in range(7):
+                    @pl.when(lower(*e_hops[out][:2], h, t))
+                    def _():
+                        e_copy(out, h, t).wait_send()
+
+    for _, blocks in E_PASSES:
+        e_pass_all(blocks, lambda copy: copy.wait_send())
+        e_pass_all(blocks, lambda copy: copy.wait_recv(), 1 - k)
 
     def finish(t, carry):
         for e in range(2):
@@ -333,12 +396,22 @@
                 def _():
                     z_copy(h, t, e).wait_send()
 
+                if e == 0:
+                    @pl.when(t > 0)
+                    def _():
+                        xf_copy(h, t, 0).wait_send()
+
                 d_copy(h, t, e).wait_send()
                 d_copy(h, t, e, 1 - k).wait_recv()
                 for m in range(2):
+                    if h == 1:
+                        @pl.when(is_side(m))
+                        def _():
+                            side_copy(m, t, e).wait_send()
+
                     @pl.when(is_source(m))
                     def _():
-                        for out in range(3):
+                        for out in range(h, 3):
                             c_copy(m, h, t, e, out, True).wait_send()
 
                     @pl.when(off_root(m))
@@ -365,7 +438,7 @@
     lax.fori_loop(0, 8, finish, 0)
 
 
-def gather(own, oth, eown, eoth):
+def gather(p4, f4, inverse_factor, diag_block):
     dma = pltpu.SemaphoreType.DMA
     return pl.pallas_call(
         comm_kernel,
@@ -379,20 +452,21 @@
         out_specs=(pl.BlockSpec(memory_space=pl.ANY),) * 4,
         scratch_shapes=[
             pltpu.VMEM((4, 4, 8, 1024), F32),
-            pltpu.VMEM((4, 4, 8, 1024), F32),
+            pltpu.VMEM((4, 4, 4, 1024), F32),
             dma((2,)), dma, dma, dma((2,)), dma((2,)),
             dma((2, 2, 7)), dma((2, 2, 7)),
             dma((2, 8, 2)), dma((2, 8, 2)),
-            dma((2, 2, 8, 2, 3)), dma((2, 2, 8, 2)),
+            dma((2, 2, 8, 2, 3)), dma((2, 2, 8, 2)), dma((2, 8, 2)),
             dma((2, 8, 2)), dma((2, 8, 2)),
+            dma((2, 8)), dma((2, 8)),
             dma((5,)),
             dma((2, 4)), dma((2, 4)),
             dma((7, 8)), dma((8, 8)),
-            dma((8,)), dma((8,)),
+            dma((8, 8)), dma((8, 8)),
         ],
         compiler_params=pltpu.CompilerParams(collective_id=0, has_side_effects=True),
         name="gather",
-    )(own, oth, eown, eoth)
+    )(p4, f4, inverse_factor, diag_block)
 
 
 def split(v):
@@ -412,7 +486,7 @@
 
 def update_kernel(pb, fb, tr, g_ref, cm_ref, cp_ref, h_ref, pown, fown, iown,
                   red_ref, panel_ref, out_ref,
-                  pc, fc, hv, ih, il, dh, dl, uh, ul, th, tl, vh, vl, sems):
+                  pc, fc, po, hv, ih, il, dh, dl, uh, ul, th, tl, vh, vl, sems):
     b = pl.program_id(0)
     a = lax.axis_index("prow")
     c = lax.axis_index("pcol")
@@ -444,21 +518,35 @@
         load_h.wait()
         for g in range(8):
             lanes = slice(128 * g, 128 * g + 128)
-            hi, lo = split(hv[0, g])
-            ih[:, lanes] = hi
-            il[:, lanes] = lo
-            hi, lo = split(hv[1, g])
-            dh[:, lanes] = hi
-            dl[:, lanes] = lo
+            deep = slice(128 * g, 1024)
+            hi, lo = split(hv[0, g, deep])
+            ih[deep, lanes] = hi
+            il[deep, lanes] = lo
+            hi, lo = split(hv[1, g, deep])
+            dh[deep, lanes] = hi
+            dl[deep, lanes] = lo
+            if g % 2 == 1:
+                top = slice(128 * g - 128, 128 * g)
+                ih[top, lanes] = jnp.zeros((128, 128), BF16)
+                il[top, lanes] = jnp.zeros((128, 128), BF16)
+            for r in range(g + 1, 8):
+                rows = slice(128 * r, 128 * r + 128)
+                hi, lo = split(hv[1, g, rows].T)
+                dh[lanes, rows] = hi
+                dl[lanes, rows] = lo
         pltpu.make_async_copy(cm_ref.at[0], pc, sems.at[0]).wait()
         pltpu.make_async_copy(cm_ref.at[0], fc, sems.at[1]).wait()
 
         hi, lo = split(fc[...].reshape(512, 1024))
         th[0:512] = hi
         tl[0:512] = lo
-        hi, lo = split(fown[...])
+        for i in range(16):
+            po[4 * i:4 * i + 4] = fown[i]
+        hi, lo = split(po[...])
         th[512:576] = hi
         tl[512:576] = lo
+        for i in range(16):
+            po[4 * i:4 * i + 4] = pown[i]
         for n in range(4):
             cols = slice(256 * n, 256 * n + 256)
             deep = slice(256 * n, 1024)
@@ -474,7 +562,7 @@
         for n in range(4):
             cols = slice(256 * n, 256 * n + 256)
             start = jnp.concatenate(
-                [pc[:, :, cols].reshape(512, 256), pown[:, cols], jnp.zeros((32, 256), F32)]
+                [pc[:, :, cols].reshape(512, 256), po[:, cols], jnp.zeros((32, 256), F32)]
             )
             t = start - dot3((uh[...], ul[...]), (dh[:, cols], dl[:, cols]), 0)
             hi, lo = split(t)
@@ -487,7 +575,8 @@
             hi, lo = split(v[0:512])
             vh[:, cols] = hi
             vl[:, cols] = lo
-            panel_ref[:, cols] = v[512:576]
+            for i in range(16):
+                panel_ref[i, :, cols] = v[512 + 4 * i:516 + 4 * i]
             red_ref[:, cols] = -v[576:608]
 
     for n in range(4):
@@ -520,19 +609,20 @@
         grid=(4,),
         out_shape=(
             jax.ShapeDtypeStruct((32, 1024), F32),
-            jax.ShapeDtypeStruct((64, 1024), F32),
+            jax.ShapeDtypeStruct((16, 4, 1024), F32),
             jax.ShapeDtypeStruct((16, 512, 128), F32),
         ),
         in_specs=[half(0), half(1), tiles, any_, any_, any_, any_,
-                  fixed((64, 1024)), fixed((64, 1024)), fixed((32, 1024))],
+                  fixed((16, 4, 1024)), fixed((16, 4, 1024)), fixed((32, 1024))],
         out_specs=(
             pl.BlockSpec((32, 1024), lambda b: (0, 0)),
-            pl.BlockSpec((64, 1024), lambda b: (0, 0)),
+            pl.BlockSpec((16, 4, 1024), lambda b: (0, 0, 0)),
             tiles,
         ),
         scratch_shapes=[
             pltpu.VMEM((4, 128, 1024), F32),
             pltpu.VMEM((4, 128, 1024), F32),
+            pltpu.VMEM((64, 1024), F32),
             pltpu.VMEM((2, 8, 1024, 128), F32),
             pltpu.VMEM((1024, 1024), BF16), pltpu.VMEM((1024, 1024), BF16),
             pltpu.VMEM((1024, 1024), BF16), pltpu.VMEM((1024, 1024), BF16),
@@ -549,24 +639,13 @@
 
 
 def body(inverse_factor, diag_block, panel_matrix, panel_factor, trailing):
-    a = lax.axis_index("prow")
-    k = lax.axis_index("pcol") % 2
-    first = k == 0
-    p4 = panel_matrix.reshape(4, 4, 4, 1024)
-    f4 = panel_factor.reshape(4, 4, 4, 1024)
-
-    def placed(v):
-        zero = jnp.zeros_like(v)
-        return jnp.concatenate([jnp.where(first, v, zero), jnp.where(first, zero, v)], axis=2)
-
-    own = placed(jnp.where(first, p4, f4))
-    oth = placed(jnp.where(first, f4, p4))
-    ei = lax.dynamic_slice_in_dim(inverse_factor, 128 * a, 128, 1)
-    ed = lax.dynamic_slice_in_dim(diag_block, 128 * a, 128, 1)
-    g, cm, cp, hh = gather(own, oth, jnp.where(first, ei, ed), jnp.where(first, ed, ei))
+    g, cm, cp, hh = gather(
+        panel_matrix.reshape(4, 4, 4, 1024), panel_factor.reshape(4, 4, 4, 1024),
+        inverse_factor, diag_block,
+    )
     red, panel, out = update(
         g, cm, cp, hh,
-        panel_matrix.reshape(64, 1024), panel_factor.reshape(64, 1024), inverse_factor,
+        panel_matrix.reshape(16, 4, 1024), panel_factor.reshape(16, 4, 1024), inverse_factor,
         trailing.reshape(16, 512, 128),
     )
     return red, panel.reshape(panel_matrix.shape), out.reshape(trailing.shape)

time: 165 us -> 146 us (0.88)
  Pallas kernels: 154 us -> 145 us
  local copies, waits for them, and re-layouts: 5.22 us -> 0 us
  other arithmetic: 3.92 us -> 0 us
    pallas_call x1, Pallas kernels: 124 us -> 114 us  [gather(): pl.pallas_call(comm_kernel, out_shape=(jax.ShapeDtypeStruct((2, 4, 4, 128...]
    reshape x3 -> x0, local copies, waits for them, and re-layouts: 5.22 us -> none  [the longest x1 1.75 us: body(): panel_factor.reshape(64, 1024)]
    select_n x2 -> x0, other arithmetic: 2.69 us -> none  [the longest x1 1.35 us: body(): jnp.where(first, ed, ei)]
where the time goes in v3:
time: 146 us
  Pallas kernels  145 us (99%)
    pallas_call x1, Pallas kernels, gather(): pl.pallas_call(comm_kernel, out_shape=(jax.ShapeDtypeStruct((2, 4, 4, 128...  114 us
    pallas_call x1, Pallas kernels, update(): pl.pallas_call(update_kernel, grid=(4,), out_shape=(jax.ShapeDtypeStruct(...  30.9 us

profile of v3, /device:TPU:15, one launch (start us, length us, event | category | flops | bytes accessed | tf_op | source)
XLA Modules:
  0.0 145.9 jit_solution(5829471348238319029)
XLA Ops:
  0.6 114.2 %gather.1 = (f32[2,4,4,128,1024]{4,3,2,1,0:T(8,128)}, f32[2,4,128,1024]{3,2,1,0:T(8,128)}, f32[4,128,1024]{2,1,0:T(8,128)}, f32[2,8,1024,128]{3,2,1,0:T(8,128)}) custom-call(f32[4,4,4,1024]{3,2,1,0:T(4,128)} %bitcast.12, f32[4,4,4,1024]{3,2,1,0:T(4,128)} %bitcast.14, f32[32,1024]{1,0:T(8,128)} %iown.1, f32[32,1024]{1,0:T(8,128)} %diag_ref.1), custom_call_target="tpu_custom_call" | custom-call | tf_op jit(solution)/shard_map/gather/pallas_call | solution.py:443
  114.8 30.9 %update.1 = (f32[32,1024]{1,0:T(8,128)}, f32[16,4,1024]{2,1,0:T(4,128)}, f32[16,512,128]{2,1,0:T(8,128)}) custom-call(f32[2,4,4,128,1024]{4,3,2,1,0:T(8,128)} %get-tuple-element.10.pb.fb.g_ref, f32[2,4,4,128,1024]{4,3,2,1,0:T(8,128)} %get-tuple-element.10.pb.fb.g_ref, f32[16,512,128]{2,1,0:T(8,128)} %bitcast.11, ...), custom_call_target="tpu_custom_call" | custom-call | tf_op jit(solution)/shard_map/update/pallas_call | solution.py:607

commit v4 on v3

--- a/solution.py
+++ b/solution.py
@@ -88,11 +88,14 @@
     def half(h):
         return merged.at[pl.ds(2 * h, 2)]
 
-    def z_ref(h, t, e):
-        return g_ref.at[k, pl.ds(2 * h, 2), pl.ds(0, 4 - e), rows8(t, h, e), :]
-
-    for h in range(2):
-        remote(half(h), z_ref(h, 0, 0), z_send.at[h, 0, 0], z_recv.at[h, 0, 0], z_to[h]).start()
+    def z_ref(h, t, e, j):
+        return g_ref.at[k, 2 * h + j, pl.ds(0, 4 - e), rows8(t, h, e), :]
+
+    for j in range(2):
+        for h in range(2):
+            remote(
+                merged.at[2 * h + j], z_ref(h, 0, 0, j), z_send.at[h, 0, j, 0], z_recv.at[h, 0, j, 0], z_to[h]
+            ).start()
 
     def far(h, e):
         ref = g_ref.at[k, pl.ds(2 * h, 2), :, rows8(0, h, e), :]
@@ -104,17 +107,22 @@
 
     for h in range(2):
         far(h, 0).start()
-    mine = [pltpu.make_async_copy(half(h), z_ref(h, 0, 0), loc_sem.at[h]) for h in range(2)]
+    mine = [
+        pltpu.make_async_copy(
+            half(h), g_ref.at[k, pl.ds(2 * h, 2), :, rows8(0, h, 0), :], loc_sem.at[h]
+        )
+        for h in range(2)
+    ]
     for h in range(2):
         mine[h].start()
 
-    def z_copy(h, t, e):
-        ref = z_ref(h, t, e)
-        return remote(ref, ref, z_send.at[h, e, t], z_recv.at[h, e, t], z_to[h])
-
-    def z_got(h, t, e):
-        ref = z_ref(h, t, e)
-        return remote(ref, ref, z_send.at[h, e, t - 1], z_recv.at[h, e, t - 1], z_to[h])
+    def z_copy(h, t, e, j):
+        ref = z_ref(h, t, e, j)
+        return remote(ref, ref, z_send.at[h, e, j, t], z_recv.at[h, e, j, t], z_to[h])
+
+    def z_got(h, t, e, j):
+        ref = z_ref(h, t, e, j)
+        return remote(ref, ref, z_send.at[h, e, j, t - 1], z_recv.at[h, e, j, t - 1], z_to[h])
 
     def d_copy(h, t, e, which=None):
         ref = g_ref.at[k if which is None else which, pl.ds(2 * h, 2), :, rows8(t, h, e), :]
@@ -321,13 +329,15 @@
     after(0, 0)
 
     def step(s, carry):
+        for j in range(2):
+            for h in range(2):
+                z_got(h, s, 0, j).wait_recv()
+
+                @pl.when(s < 7)
+                def _():
+                    z_copy(h, s, 0, j).start()
+
         for h in range(2):
-            z_got(h, s, 0).wait_recv()
-
-            @pl.when(s < 7)
-            def _():
-                z_copy(h, s, 0).start()
-
             xf_copy(h, s, 0).start()
 
         after(s, 0)
@@ -340,11 +350,13 @@
             def _():
                 far(h, 1).wait_recv()
 
-            @pl.when(t > 0)
-            def _():
-                z_got(h, jnp.maximum(t, 1), 1).wait_recv()
-
-            z_copy(h, t, 1).start()
+        for j in range(2):
+            for h in range(2):
+                @pl.when(t > 0)
+                def _():
+                    z_got(h, jnp.maximum(t, 1), 1, j).wait_recv()
+
+                z_copy(h, t, 1, j).start()
 
         for h in range(2):
             @pl.when(t > 0)
@@ -359,7 +371,8 @@
     lax.fori_loop(1, 8, step, 0)
     last = jnp.int32(7)
     for h in range(2):
-        z_got(h, last, 1).wait_recv()
+        for j in range(2):
+            z_got(h, last, 1, j).wait_recv()
         xf_copy(h, last, 1).wait_recv()
     after(last, 1)
     for lag in (1, 2, 3):
@@ -394,7 +407,8 @@
             for h in range(2):
                 @pl.when(t < 7)
                 def _():
-                    z_copy(h, t, e).wait_send()
+                    for j in range(2):
+                        z_copy(h, t, e, j).wait_send()
 
                 if e == 0:
                     @pl.when(t > 0)
@@ -454,7 +468,7 @@
             pltpu.VMEM((4, 4, 8, 1024), F32),
             pltpu.VMEM((4, 4, 4, 1024), F32),
             dma((2,)), dma, dma, dma((2,)), dma((2,)),
-            dma((2, 2, 7)), dma((2, 2, 7)),
+            dma((2, 2, 2, 7)), dma((2, 2, 2, 7)),
             dma((2, 8, 2)), dma((2, 8, 2)),
             dma((2, 2, 8, 2, 3)), dma((2, 2, 8, 2)), dma((2, 8, 2)),
             dma((2, 8, 2)), dma((2, 8, 2)),
@@ -484,19 +498,33 @@
 ROWS = 608
 
 
-def update_kernel(pb, fb, tr, g_ref, cm_ref, cp_ref, h_ref, pown, fown, iown,
+def update_kernel(tr, g_ref, cm_ref, cp_ref, h_ref, pown, fown, iown,
                   red_ref, panel_ref, out_ref,
-                  pc, fc, po, hv, ih, il, dh, dl, uh, ul, th, tl, vh, vl, sems):
+                  pb, fb, pc, fc, po, hv, ih, il, dh, dl, uh, ul, th, tl, vh, vl, sems):
     b = pl.program_id(0)
     a = lax.axis_index("prow")
     c = lax.axis_index("pcol")
     z, xh, k = c // 4, (c // 2) % 2, c % 2
     source = a == (z % 2) * 4 + 2 * xh + k
 
+    def stream(n):
+        return [
+            pltpu.make_async_copy(g_ref.at[w, n], (pb, fb)[w].at[n % 2], sems.at[2 + 2 * w + n % 2])
+            for w in range(2)
+        ]
+
+    def slices(g):
+        deep = pl.ds(128 * g, 1024 - 128 * g)
+        return [
+            pltpu.make_async_copy(h_ref.at[w, g, deep], hv.at[w, g, deep], sems.at[6 + 8 * w + g])
+            for w in range(2)
+        ]
+
     @pl.when(b == 0)
     def _():
-        load_h = pltpu.make_async_copy(h_ref, hv, sems.at[2])
-        load_h.start()
+        for g in range(8):
+            for copy in slices(g):
+                copy.start()
 
         @pl.when(source)
         def _():
@@ -515,10 +543,14 @@
                 pltpu.make_async_copy(cp_ref, pc, sems.at[0]).start()
                 pltpu.make_async_copy(cm_ref.at[1], fc, sems.at[1]).start()
 
-        load_h.wait()
+        for n in range(2):
+            for copy in stream(n):
+                copy.start()
         for g in range(8):
             lanes = slice(128 * g, 128 * g + 128)
             deep = slice(128 * g, 1024)
+            for copy in slices(g):
+                copy.wait()
             hi, lo = split(hv[0, g, deep])
             ih[deep, lanes] = hi
             il[deep, lanes] = lo
@@ -582,10 +614,15 @@
     for n in range(4):
         @pl.when(b == n)
         def _():
+            if 0 < n < 3:
+                for copy in stream(n + 1):
+                    copy.start()
+            for copy in stream(n):
+                copy.wait()
             wide = slice(0, 128 * n + 128)
             for q in range(2):
-                first = split(pb[0, 0, 2 * q:2 * q + 2].reshape(256, 1024))
-                second = split(fb[0, 0, 2 * q:2 * q + 2].reshape(256, 1024))
+                first = split(pb[n % 2, 2 * q:2 * q + 2].reshape(256, 1024))
+                second = split(fb[n % 2, 2 * q:2 * q + 2].reshape(256, 1024))
                 total = dot3(first, (uh[wide], ul[wide]), 1) + dot3(second, (vh[wide], vl[wide]), 1)
                 for p in range(2):
                     i = 2 * q + p
@@ -602,7 +639,6 @@
 def update(g, cm, cp, hh, pown, fown, iown, trailing):
     any_ = pl.BlockSpec(memory_space=pl.ANY)
     fixed = lambda shape: pl.BlockSpec(shape, lambda b: (0,) * len(shape), pipeline_mode=pl.Buffered(1))
-    half = lambda which: pl.BlockSpec((1, 1, 4, 128, 1024), lambda b: (which, b, 0, 0, 0))
     tiles = pl.BlockSpec((4, 512, 128), lambda b: (b, 0, 0))
     return pl.pallas_call(
         update_kernel,
@@ -612,7 +648,7 @@
             jax.ShapeDtypeStruct((16, 4, 1024), F32),
             jax.ShapeDtypeStruct((16, 512, 128), F32),
         ),
-        in_specs=[half(0), half(1), tiles, any_, any_, any_, any_,
+        in_specs=[tiles, any_, any_, any_, any_,
                   fixed((16, 4, 1024)), fixed((16, 4, 1024)), fixed((32, 1024))],
         out_specs=(
             pl.BlockSpec((32, 1024), lambda b: (0, 0)),
@@ -620,6 +656,8 @@
             tiles,
         ),
         scratch_shapes=[
+            pltpu.VMEM((2, 4, 128, 1024), F32),
+            pltpu.VMEM((2, 4, 128, 1024), F32),
             pltpu.VMEM((4, 128, 1024), F32),
             pltpu.VMEM((4, 128, 1024), F32),
             pltpu.VMEM((64, 1024), F32),
@@ -629,13 +667,13 @@
             pltpu.VMEM((ROWS, 1024), BF16), pltpu.VMEM((ROWS, 1024), BF16),
             pltpu.VMEM((ROWS, 1024), BF16), pltpu.VMEM((ROWS, 1024), BF16),
             pltpu.VMEM((512, 1024), BF16), pltpu.VMEM((512, 1024), BF16),
-            pltpu.SemaphoreType.DMA((3,)),
+            pltpu.SemaphoreType.DMA((22,)),
         ],
         compiler_params=pltpu.CompilerParams(
             dimension_semantics=("arbitrary",), vmem_limit_bytes=63 * 1024 * 1024
         ),
         name="update",
-    )(g, g, trailing, g, cm, cp, hh, pown, fown, iown)
+    )(trailing, g, cm, cp, hh, pown, fown, iown)
 
 
 def body(inverse_factor, diag_block, panel_matrix, panel_factor, trailing):

time: 146 us -> 143 us (0.979)
  Pallas kernels: 145 us -> 141 us
    pallas_call x1, Pallas kernels: 30.9 us -> 27.3 us  [update(): pl.pallas_call(update_kernel, grid=(4,), out_shape=(jax.ShapeDtypeStruct(...]
where the time goes in v4:
time: 143 us; the launch traced here: 142 us
  Pallas kernels  141 us (99%)
    pallas_call x1, Pallas kernels, gather(): pl.pallas_call(comm_kernel, out_shape=(jax.ShapeDtypeStruct((2, 4, 4, 128...  113 us
    pallas_call x1, Pallas kernels, update(): pl.pallas_call(update_kernel, grid=(4,), out_shape=(jax.ShapeDtypeStruct(...  27.3 us

profile of v4, /device:TPU:15, one launch (start us, length us, event | category | flops | bytes accessed | tf_op | source)
XLA Modules:
  0.0 141.5 jit_solution(3646556179950606325)
XLA Ops:
  0.6 113.4 %gather.1 = (f32[2,4,4,128,1024]{4,3,2,1,0:T(8,128)}, f32[2,4,128,1024]{3,2,1,0:T(8,128)}, f32[4,128,1024]{2,1,0:T(8,128)}, f32[2,8,1024,128]{3,2,1,0:T(8,128)}) custom-call(f32[4,4,4,1024]{3,2,1,0:T(4,128)} %bitcast.12, f32[4,4,4,1024]{3,2,1,0:T(4,128)} %bitcast.14, f32[32,1024]{1,0:T(8,128)} %iown.1, f32[32,1024]{1,0:T(8,128)} %diag_ref.1), custom_call_target="tpu_custom_call" | custom-call | tf_op jit(solution)/shard_map/gather/pallas_call | solution.py:457
  114.1 27.3 %update.1 = (f32[32,1024]{1,0:T(8,128)}, f32[16,4,1024]{2,1,0:T(4,128)}, f32[16,512,128]{2,1,0:T(8,128)}) custom-call(f32[16,512,128]{2,1,0:T(8,128)} %bitcast.11, f32[2,4,4,128,1024]{4,3,2,1,0:T(8,128)} %get-tuple-element.10.g_ref, f32[2,4,128,1024]{3,2,1,0:T(8,128)} %get-tuple-element.11.cm_ref, f32[4,128,1024]{2,1,0:T(8,128)} %get-tuple-element.12.cp_ref, ...), custom_call_target="tpu_custom_call" | custom-call | tf_op jit(solution)/shard_map/update/pallas_call | solution.py:643

commit v5 on v4

--- a/solution.py
+++ b/solution.py
@@ -94,7 +94,7 @@
     for j in range(2):
         for h in range(2):
             remote(
-                merged.at[2 * h + j], z_ref(h, 0, 0, j), z_send.at[h, 0, j, 0], z_recv.at[h, 0, j, 0], z_to[h]
+                merged.at[2 * h + j], z_ref(h, 0, 0, j), z_send.at[0], z_recv.at[h, 0, j, 0], z_to[h]
             ).start()
 
     def far(h, e):
@@ -103,7 +103,7 @@
 
     def xf_copy(h, t, e):
         ref = g_ref.at[k, pl.ds(2 * h, 2), pl.ds(3, 1), rows8(t, h, e), :]
-        return remote(ref, ref, xf_send.at[h, t], xf_recv.at[h, t], x_far)
+        return remote(ref, ref, xf_send, xf_recv.at[h, t], x_far)
 
     for h in range(2):
         far(h, 0).start()
@@ -118,15 +118,15 @@
 
     def z_copy(h, t, e, j):
         ref = z_ref(h, t, e, j)
-        return remote(ref, ref, z_send.at[h, e, j, t], z_recv.at[h, e, j, t], z_to[h])
+        return remote(ref, ref, z_send.at[e], z_recv.at[h, e, j, t], z_to[h])
 
     def z_got(h, t, e, j):
         ref = z_ref(h, t, e, j)
-        return remote(ref, ref, z_send.at[h, e, j, t - 1], z_recv.at[h, e, j, t - 1], z_to[h])
+        return remote(ref, ref, z_send.at[e], z_recv.at[h, e, j, t - 1], z_to[h])
 
     def d_copy(h, t, e, which=None):
         ref = g_ref.at[k if which is None else which, pl.ds(2 * h, 2), :, rows8(t, h, e), :]
-        return remote(ref, ref, d_send.at[h, t, e], d_recv.at[h, t, e], partner)
+        return remote(ref, ref, d_send, d_recv, partner)
 
     def e_rows(which, dx, dy, h, t):
         block = lax.rem(xl + dx, 2) * 4 + lax.rem(y + dy, 4)
@@ -240,12 +240,12 @@
         dst = cm_ref.at[m, pl.ds(2 * h, 2), rows8(t, h, e), :]
         src = g_ref.at[k, pl.ds(2 * h, 2), q, rows8(t, h, e), :] if from_g else dst
         to = (x_near, y_next, y_prev)[out]
-        return remote(src, dst, c_send.at[m, h, t, e, out], c_recv.at[m, h, t, e], to)
+        return remote(src, dst, c_send.at[m, out], c_recv.at[m, h, t, e], to)
 
     def cd_copy(m, h, t, e):
         src = cm_ref.at[m, pl.ds(2 * h, 2), rows8(t, h, e), :]
         dst = cp_ref.at[pl.ds(2 * h, 2), rows8(t, h, e), :]
-        return remote(src, dst, cd_send.at[h, t, e], cd_recv.at[h, t, e], partner)
+        return remote(src, dst, cd_send, cd_recv, partner)
 
     def is_source(m):
         return jnp.logical_and(in_plane, place(m) == 0)
@@ -262,7 +262,7 @@
     def side_copy(m, t, e):
         src = g_ref.at[k, pl.ds(2, 2), q, rows8(t, 1, e), :]
         dst = cm_ref.at[m, pl.ds(2, 2), rows8(t, 1, e), :]
-        return remote(src, dst, cf_send.at[m, t, e], c_recv.at[m, 1, t, 1 - e], x_side)
+        return remote(src, dst, cf_send.at[m], c_recv.at[m, 1, t, 1 - e], x_side)
 
     def source_sends(t, e):
         for m in range(2):
@@ -309,9 +309,9 @@
                         cd_copy(m, h, s, e).start()
 
     def after(t, e):
+        source_sends(t, e)
         for h in range(2):
             d_copy(h, t, e).start()
-        source_sends(t, e)
 
     mine[0].wait()
     mine[1].wait()
@@ -402,54 +402,45 @@
         e_pass_all(blocks, lambda copy: copy.wait_send())
         e_pass_all(blocks, lambda copy: copy.wait_recv(), 1 - k)
 
-    def finish(t, carry):
-        for e in range(2):
-            for h in range(2):
-                @pl.when(t < 7)
-                def _():
-                    for j in range(2):
-                        z_copy(h, t, e, j).wait_send()
-
-                if e == 0:
-                    @pl.when(t > 0)
-                    def _():
-                        xf_copy(h, t, 0).wait_send()
-
-                d_copy(h, t, e).wait_send()
-                d_copy(h, t, e, 1 - k).wait_recv()
-                for m in range(2):
-                    if h == 1:
-                        @pl.when(is_side(m))
-                        def _():
-                            side_copy(m, t, e).wait_send()
-
-                    @pl.when(is_source(m))
-                    def _():
-                        for out in range(h, 3):
-                            c_copy(m, h, t, e, out, True).wait_send()
-
-                    @pl.when(off_root(m))
-                    def _():
-                        for out in (1, 2):
-                            c_copy(m, h, t, e, out).wait_send()
-
-                    @pl.when(relays(m))
-                    def _():
-                        c_copy(m, h, t, e, y_out[m]).wait_send()
-
-                    @pl.when(jnp.logical_not(is_source(m)))
-                    def _():
-                        @pl.when(k != m)
-                        def _():
-                            cd_copy(m, h, t, e).wait_send()
-
-                        @pl.when(k == m)
-                        def _():
-                            cd_copy(m, h, t, e).wait_recv()
-
-        return carry
-
-    lax.fori_loop(0, 8, finish, 0)
+    def sent(ref, sem):
+        remote(ref, ref, sem, xh_recv.at[0], partner).wait_send()
+
+    steps = pl.ds(0, 112)
+    sent(g_ref.at[k, pl.ds(0, 2), :, steps, :], z_send.at[0])
+    sent(g_ref.at[k, pl.ds(0, 2), pl.ds(0, 3), steps, :], z_send.at[1])
+    sent(g_ref.at[k, pl.ds(0, 2), pl.ds(0, 1), steps, :], xf_send)
+    for m in range(2):
+        whole, part = cm_ref.at[m], cm_ref.at[m, pl.ds(0, 2)]
+
+        @pl.when(is_side(m))
+        def _():
+            sent(part, cf_send.at[m])
+
+        @pl.when(is_source(m))
+        def _():
+            sent(part, c_send.at[m, 0])
+
+        @pl.when(place(m) == 0)
+        def _():
+            for out in (1, 2):
+                sent(whole, c_send.at[m, out])
+
+        @pl.when(relays(m))
+        def _():
+            sent(whole, c_send.at[m, y_out[m]])
+
+        @pl.when(jnp.logical_not(is_source(m)))
+        def _():
+            @pl.when(k != m)
+            def _():
+                sent(cp_ref, cd_send)
+
+            @pl.when(k == m)
+            def _():
+                remote(cp_ref, cp_ref, cd_send, cd_recv, partner).wait_recv()
+
+    sent(g_ref.at[k], d_send)
+    remote(g_ref.at[1 - k], g_ref.at[1 - k], d_send, d_recv, partner).wait_recv()
 
 
 def gather(p4, f4, inverse_factor, diag_block):
@@ -468,11 +459,11 @@
             pltpu.VMEM((4, 4, 8, 1024), F32),
             pltpu.VMEM((4, 4, 4, 1024), F32),
             dma((2,)), dma, dma, dma((2,)), dma((2,)),
-            dma((2, 2, 2, 7)), dma((2, 2, 2, 7)),
-            dma((2, 8, 2)), dma((2, 8, 2)),
-            dma((2, 2, 8, 2, 3)), dma((2, 2, 8, 2)), dma((2, 8, 2)),
-            dma((2, 8, 2)), dma((2, 8, 2)),
-            dma((2, 8)), dma((2, 8)),
+            dma((2,)), dma((2, 2, 2, 7)),
+            dma, dma,
+            dma((2, 3)), dma((2, 2, 8, 2)), dma((2,)),
+            dma, dma,
+            dma, dma((2, 8)),
             dma((5,)),
             dma((2, 4)), dma((2, 4)),
             dma((7, 8)), dma((8, 8)),

time: 143 us -> 139 us (0.972)
  Pallas kernels: 141 us -> 137 us
    pallas_call x1, Pallas kernels: 113 us -> 110 us  [gather(): pl.pallas_call(comm_kernel, out_shape=(jax.ShapeDtypeStruct((2, 4, 4, 128...]
where the time goes in v5:
time: 139 us; the launch traced here: 138 us
  Pallas kernels  137 us (99%)
    pallas_call x1, Pallas kernels, gather(): pl.pallas_call(comm_kernel, out_shape=(jax.ShapeDtypeStruct((2, 4, 4, 128...  110 us
    pallas_call x1, Pallas kernels, update(): pl.pallas_call(update_kernel, grid=(4,), out_shape=(jax.ShapeDtypeStruct(...  27.3 us

profile of v5, /device:TPU:15, one launch (start us, length us, event | category | flops | bytes accessed | tf_op | source)
XLA Modules:
  0.0 137.8 jit_solution(11200552983870980066)
XLA Ops:
  0.6 109.7 %gather.1 = (f32[2,4,4,128,1024]{4,3,2,1,0:T(8,128)}, f32[2,4,128,1024]{3,2,1,0:T(8,128)}, f32[4,128,1024]{2,1,0:T(8,128)}, f32[2,8,1024,128]{3,2,1,0:T(8,128)}) custom-call(f32[4,4,4,1024]{3,2,1,0:T(4,128)} %bitcast.12, f32[4,4,4,1024]{3,2,1,0:T(4,128)} %bitcast.14, f32[32,1024]{1,0:T(8,128)} %iown.1, f32[32,1024]{1,0:T(8,128)} %diag_ref.1), custom_call_target="tpu_custom_call" | custom-call | tf_op jit(solution)/shard_map/gather/pallas_call | solution.py:448
  110.4 27.3 %update.1 = (f32[32,1024]{1,0:T(8,128)}, f32[16,4,1024]{2,1,0:T(4,128)}, f32[16,512,128]{2,1,0:T(8,128)}) custom-call(f32[16,512,128]{2,1,0:T(8,128)} %bitcast.11, f32[2,4,4,128,1024]{4,3,2,1,0:T(8,128)} %get-tuple-element.10.g_ref, f32[2,4,128,1024]{3,2,1,0:T(8,128)} %get-tuple-element.11.cm_ref, f32[4,128,1024]{2,1,0:T(8,128)} %get-tuple-element.12.cp_ref, ...), custom_call_target="tpu_custom_call" | custom-call | tf_op jit(solution)/shard_map/update/pallas_call | solution.py:634

commit v6 on v5

--- a/solution.py
+++ b/solution.py
@@ -216,7 +216,7 @@
 
     def e_piece(dx, dy, p, which):
         ref = h_rows(which, blk(dx, dy), 128 * p, 128)
-        return remote(ref, ref, ed_send.at[4 * dx + dy, p], ed_recv.at[4 * dx + dy, p], partner)
+        return remote(ref, ref, ed_send, ed_recv, partner)
 
     def e_pass_all(blocks, act, which=None):
         def piece(p, carry):
@@ -398,10 +398,6 @@
                     def _():
                         e_copy(out, h, t).wait_send()
 
-    for _, blocks in E_PASSES:
-        e_pass_all(blocks, lambda copy: copy.wait_send())
-        e_pass_all(blocks, lambda copy: copy.wait_recv(), 1 - k)
-
     def sent(ref, sem):
         remote(ref, ref, sem, xh_recv.at[0], partner).wait_send()
 
@@ -439,6 +435,9 @@
             def _():
                 remote(cp_ref, cp_ref, cd_send, cd_recv, partner).wait_recv()
 
+    deep = pl.ds(0, 576)
+    sent(h_ref.at[k, :, deep, :], ed_send)
+    remote(h_ref.at[1 - k, :, deep, :], h_ref.at[1 - k, :, deep, :], ed_send, ed_recv, partner).wait_recv()
     sent(g_ref.at[k], d_send)
     remote(g_ref.at[1 - k], g_ref.at[1 - k], d_send, d_recv, partner).wait_recv()
 
@@ -467,7 +466,7 @@
             dma((5,)),
             dma((2, 4)), dma((2, 4)),
             dma((7, 8)), dma((8, 8)),
-            dma((8, 8)), dma((8, 8)),
+            dma, dma,
         ],
         compiler_params=pltpu.CompilerParams(collective_id=0, has_side_effects=True),
         name="gather",

time: 139 us -> 138 us (level)
  no operation moved by 1% of the time
where the time goes in v6:
time: 138 us; the launch traced here: 137 us
  Pallas kernels  136 us (99%)
    pallas_call x1, Pallas kernels, gather(): pl.pallas_call(comm_kernel, out_shape=(jax.ShapeDtypeStruct((2, 4, 4, 128...  109 us
    pallas_call x1, Pallas kernels, update(): pl.pallas_call(update_kernel, grid=(4,), out_shape=(jax.ShapeDtypeStruct(...  27.3 us

profile of v6, /device:TPU:15, one launch (start us, length us, event | category | flops | bytes accessed | tf_op | source)
XLA Modules:
  0.0 136.7 jit_solution(1905185486121794869)
XLA Ops:
  0.6 108.6 %gather.1 = (f32[2,4,4,128,1024]{4,3,2,1,0:T(8,128)}, f32[2,4,128,1024]{3,2,1,0:T(8,128)}, f32[4,128,1024]{2,1,0:T(8,128)}, f32[2,8,1024,128]{3,2,1,0:T(8,128)}) custom-call(f32[4,4,4,1024]{3,2,1,0:T(4,128)} %bitcast.12, f32[4,4,4,1024]{3,2,1,0:T(4,128)} %bitcast.14, f32[32,1024]{1,0:T(8,128)} %iown.1, f32[32,1024]{1,0:T(8,128)} %diag_ref.1), custom_call_target="tpu_custom_call" | custom-call | tf_op jit(solution)/shard_map/gather/pallas_call | solution.py:447
  109.3 27.3 %update.1 = (f32[32,1024]{1,0:T(8,128)}, f32[16,4,1024]{2,1,0:T(4,128)}, f32[16,512,128]{2,1,0:T(8,128)}) custom-call(f32[16,512,128]{2,1,0:T(8,128)} %bitcast.11, f32[2,4,4,128,1024]{4,3,2,1,0:T(8,128)} %get-tuple-element.10.g_ref, f32[2,4,128,1024]{3,2,1,0:T(8,128)} %get-tuple-element.11.cm_ref, f32[4,128,1024]{2,1,0:T(8,128)} %get-tuple-element.12.cp_ref, ...), custom_call_target="tpu_custom_call" | custom-call | tf_op jit(solution)/shard_map/update/pallas_call | solution.py:633
